TPU v7x, 32 devices: a whole 2x2x4 slice. The times are simulated.
32 devices in a mesh: groups: 2 (over x), expert: 8 (over z, y), mp: 2 (over core).
Axes of the slice: x: 2, y: 2, z: 4, core: 2. Of those that a mesh axis runs over, the one named last changes fastest.
Arguments:
- residual: bfloat16 [512, 5120], P(('groups', 'expert'), 'mp'), parts along dimension 0, may hold values from -6 to 6
- norm_gain: bfloat16 [5120], P('mp'), may hold values from 0.099609375 to 1.8984375
- router_weight: bfloat16 [640, 128], replicated, may hold values from -0.25 to 0.25
- expert_ids: int32 [512, 8, 2], P(('groups', 'expert')), parts along dimension 0, may hold values from 0 to 127, all different within a row; in each aligned block of 256 rows (0 to 255, 256 to 511, ..., all dimensions but the last counted through in order) at most 5 rows name the same one
- expert_in: bfloat16 [128, 640, 1280], P('expert', None, 'mp'), may hold values from -0.25 to 0.25
- expert_out: bfloat16 [128, 1280, 640], P('expert', 'mp'), may hold values from -0.15625 to 0.15625
- queries: bfloat16 [512, 5120], P(('groups', 'expert'), 'mp'), parts along dimension 0, may hold values from -6 to 6
- new_keys: bfloat16 [512, 1024], P(('groups', 'expert'), 'mp'), parts along dimension 0, may hold values from -6 to 6
- new_values: bfloat16 [512, 1024], P(('groups', 'expert'), 'mp'), parts along dimension 0, may hold values from -6 to 6
- cache_keys: bfloat16 [512, 128, 1024], P(('groups', 'expert'), None, 'mp'), parts along dimension 0, may hold values from -6 to 6
- cache_values: bfloat16 [512, 128, 1024], P(('groups', 'expert'), None, 'mp'), parts along dimension 0, may hold values from -6 to 6
- lengths: int32 [512], P(('groups', 'expert')), parts along dimension 0, may hold values from 1 to 128
Outputs:
- attention: bfloat16 [512, 5120], P(('groups', 'expert'), 'mp'), parts along dimension 0
- mixed: bfloat16 [512, 5120], P(('groups', 'expert'), 'mp'), parts along dimension 0
There are 2 independent parts, one for each index of `groups`. A program takes and returns all parts, laid end to end along the dimension named above; an argument that names none is the same for every part. Nothing has to cross between parts.
Inputs may be any that keep to these rules, and one draw needn't show every extreme that they name: `expert_ids`: within the 8 sub-tokens of each aligned block of 32 tokens, no expert is named more than 5 times, a bound that some block reaches; the 2 experts of one sub-token differ.
All inputs are finite; a program needn't handle non-finite values.
Results may differ from a plain program's by a relative error of at most 0.006.
Values may be sent and summed in bfloat16 or wider, within the bound.
No kernel may reach another device: no remote copies, remote signals or barrier semaphores. Data moves between devices by JAX's collectives and lax.ppermute only.
A program may use at most 128 MiB of HBM per device.

v0:
```python
import math

import jax
import jax.numpy as jnp
from jax import lax
from jax.sharding import PartitionSpec as P

D = 5120
SUB = 8
HEADS = 40
HD = 128
KV_HEADS = 8
EXPERTS = 128
TOP = 2
CAP = 5


def expert_ffn(received, first_weight, second_weight):
    hidden = jax.nn.gelu(
        jnp.einsum("scew,ewf->scef", received, first_weight, preferred_element_type=jnp.float32)
    ).astype(jnp.bfloat16)
    return jnp.einsum("scef,efw->scew", hidden, second_weight, preferred_element_type=jnp.float32)


def attend(queries, new_keys, new_values, cache_keys, cache_values, lengths):
    tokens = queries.shape[0]
    per_group = HEADS // KV_HEADS
    groups = new_keys.shape[1] // HD
    cache_len = cache_keys.shape[1]
    score_scale = 1.0 / math.sqrt(HD)
    query_heads = queries.reshape(tokens, groups, per_group, HD)
    keys_old = cache_keys.reshape(tokens, cache_len, groups, HD)
    values_old = cache_values.reshape(tokens, cache_len, groups, HD)
    keys_new = new_keys.reshape(tokens, groups, HD)
    values_new = new_values.reshape(tokens, groups, HD)
    scores = (
        jnp.einsum("tgqd,tjgd->tgqj", query_heads, keys_old, preferred_element_type=jnp.float32)
        * score_scale
    )
    fresh_score = (
        jnp.einsum("tgqd,tgd->tgq", query_heads, keys_new, preferred_element_type=jnp.float32)
        * score_scale
    )
    usable = (jnp.arange(cache_len, dtype=jnp.int32)[None, :] < lengths[:, None])[:, None, None, :]
    scores = jnp.where(usable, scores, -1e30)
    row_max = jnp.maximum(jnp.max(scores, axis=-1), fresh_score)
    expo_old = jnp.where(usable, jnp.exp(scores - row_max[..., None]), 0.0)
    expo_new = jnp.exp(fresh_score - row_max)
    totals = jnp.sum(expo_old, axis=-1) + expo_new
    cache_probs = (expo_old / totals[..., None]).astype(jnp.bfloat16)
    fresh_probs = (expo_new / totals).astype(jnp.bfloat16)
    context = jnp.einsum(
        "tgqj,tjgd->tgqd", cache_probs, values_old, preferred_element_type=jnp.float32
    )
    context = (
        context
        + fresh_probs.astype(jnp.float32)[..., None] * values_new.astype(jnp.float32)[:, :, None, :]
    )
    return context.reshape(tokens, groups * per_group * HD)


def per_device(
    residual,
    norm_gain,
    router_weight,
    expert_ids,
    expert_in,
    expert_out,
    queries,
    new_keys,
    new_values,
    cache_keys,
    cache_values,
    lengths,
):
    sub_width = D // SUB
    tokens = residual.shape[0]
    sub_local = residual.shape[1] // sub_width
    expert_count = lax.axis_size("expert")
    mp_count = lax.axis_size("mp")
    per_owner = expert_in.shape[0]
    pieces = residual.astype(jnp.float32).reshape(tokens, sub_local, sub_width)
    gain_rows = norm_gain.astype(jnp.float32).reshape(sub_local, sub_width)
    meansq = jnp.mean(pieces * pieces, axis=-1, keepdims=True)
    normed = (pieces * lax.rsqrt(meansq + 1e-06) * gain_rows).astype(jnp.bfloat16)
    own_ids = lax.dynamic_slice_in_dim(expert_ids, lax.axis_index("mp") * sub_local, sub_local, 1)
    logits = jnp.einsum("tsw,we->tse", normed, router_weight, preferred_element_type=jnp.float32)
    expert_range = jnp.arange(EXPERTS, dtype=jnp.int32)
    chosen = (own_ids[..., None] == expert_range).astype(jnp.float32)
    picked_logits = jnp.sum(chosen * logits[:, :, None, :], axis=-1)
    gate_scores = jax.nn.sigmoid(picked_logits)
    weights = gate_scores / jnp.sum(gate_scores, axis=-1, keepdims=True)
    flat_ids = own_ids.reshape(-1)
    choice_count = flat_ids.shape[0]
    onehot = (flat_ids[:, None] == expert_range[None, :]).astype(jnp.bfloat16)
    positions = jnp.arange(choice_count, dtype=jnp.int32)
    earlier = (positions[:, None] > positions[None, :]).astype(jnp.bfloat16)
    before = jnp.dot(earlier, onehot, preferred_element_type=jnp.float32)
    slot_index = jnp.sum(before * onehot.astype(jnp.float32), axis=1).astype(jnp.int32)
    owner_index = flat_ids // per_owner
    local_index = flat_ids % per_owner
    flat_index = (owner_index * CAP + slot_index) * per_owner + local_index
    dispatch = (flat_index[:, None] == jnp.arange(EXPERTS * CAP, dtype=jnp.int32)[None, :]).astype(
        jnp.bfloat16
    )
    sources = jnp.broadcast_to(normed[:, :, None, :], (tokens, sub_local, TOP, sub_width)).reshape(
        choice_count, sub_width
    )
    outgoing = jnp.einsum(
        "cs,cw->sw", dispatch, sources, preferred_element_type=jnp.float32
    ).astype(jnp.bfloat16)
    outgoing = outgoing.reshape(expert_count, CAP, per_owner, sub_width)
    copies = jnp.broadcast_to(
        outgoing[:, None], (expert_count, mp_count, CAP, per_owner, sub_width)
    )
    copies = copies.reshape(expert_count * mp_count, CAP, per_owner, sub_width)
    partial_value = expert_ffn(
        lax.all_to_all(copies, ("expert", "mp"), split_axis=0, concat_axis=0, tiled=True),
        expert_in,
        expert_out,
    )
    partials = lax.all_to_all(
        partial_value.astype(jnp.bfloat16),
        ("expert", "mp"),
        split_axis=0,
        concat_axis=0,
        tiled=True,
    ).astype(partial_value.dtype)
    partials = partials.reshape(expert_count, mp_count, CAP, per_owner, sub_width)
    returned = jnp.sum(partials, axis=1).astype(jnp.bfloat16)
    picked = jnp.dot(
        dispatch, returned.reshape(EXPERTS * CAP, sub_width), preferred_element_type=jnp.float32
    )
    picked = picked.reshape(tokens, sub_local, TOP, sub_width)
    moe = jnp.sum(weights[..., None] * picked, axis=2).reshape(tokens, sub_local * sub_width)
    context = attend(queries, new_keys, new_values, cache_keys, cache_values, lengths)
    attention = context.astype(jnp.bfloat16)
    mixed = (residual.astype(jnp.float32) + context + moe).astype(jnp.bfloat16)
    return (attention, mixed)


def solution(mesh):
    placed = (
        P(("groups", "expert"), "mp"),
        P("mp"),
        P(),
        P(("groups", "expert"), None, None),
        P("expert", None, "mp"),
        P("expert", "mp", None),
        P(("groups", "expert"), "mp"),
        P(("groups", "expert"), "mp"),
        P(("groups", "expert"), "mp"),
        P(("groups", "expert"), None, "mp"),
        P(("groups", "expert"), None, "mp"),
        P(("groups", "expert")),
    )
    return jax.shard_map(
        per_device,
        mesh=mesh,
        in_specs=placed,
        out_specs=(P(("groups", "expert"), "mp"), P(("groups", "expert"), "mp")),
        check_vma=False,
    )
```

profile of v0, /device:TPU:13, one launch (start us, length us, event | category | flops | bytes accessed | tf_op | source)
XLA Modules:
  0.0 106.2 jit_solution(4366529445903931518)
XLA Ops:
  0.6 0.0 copy-start
  0.6 1.1 reshape.189
  1.7 0.1 multiply_reduce_fusion
  1.9 0.7 reshape.196
  2.6 0.7 constant_dynamic-slice_fusion
  3.3 0.1 copy.78
  3.4 0.1 eq.68
  3.5 0.2 fusion.37
  3.8 0.1 multiply_convert_fusion
  3.9 0.2 broadcast_in_dim.23
  4.1 0.1 reshape.190
  4.3 0.6 convolution_convert_fusion
  4.9 0.1 broadcast_in_dim.29
  5.0 43.9 %all_to_all.10 = bf16[16,5,16,640]{3,2,1,0:T(8,128)(2,1)S(1)} all-to-all(bf16[16,5,16,640]{3,2,1,0:T(8,128)(2,1)S(1)} %bitcast.67), channel_id=1, replica_groups=mesh['groups'=2,'expert'=8,'mp'=2] {'expert','mp'}, dimensions={0} | all-to-all | bytes 3276800 | tf_op jit(solution)/shard_map/all_to_all | solution.py:118
  48.9 0.0 copy-start.1
  48.9 7.5 %fusion.17 = bf16[16,5,16,640]{3,0,1,2:T(8,128)(2,1)S(1)} fusion(bf16[16,640,640]{2,1,0:T(8,128)(2,1)} %param.16, bf16[16,5,16,640]{3,2,1,0:T(8,128)(2,1)S(1)} %all_to_all.10), kind=kOutput, calls=%fused_computation.18 | convolution fusion | flops 1055948800 | bytes 16384000 | tf_op jit(solution)/shard_map/scew,ewf->scef/dot_general | solution.py:20
  56.4 0.9 copy-done.1
  57.3 2.4 %fusion.24 = bf16[16,5,16,640]{3,0,1,2:T(8,128)(2,1)S(1)} fusion(bf16[16,5,16,640]{3,0,1,2:T(8,128)(2,1)S(1)} %fusion.17, bf16[16,640,640]{2,1,0:T(8,128)(2,1)S(1)} %copy-done.1), kind=kOutput, calls=%fused_computation.22 | convolution fusion | flops 1049395200 | bytes 16384000 | tf_op jit(solution)/shard_map/scef,efw->scew/dot_general | solution.py:22
  59.7 0.0 copy-start.3
  59.7 0.0 copy-start.4
  59.7 0.0 copy-start.5
  59.8 0.0 copy-start.6
  59.8 1.5 %copy.82 = bf16[16,5,16,640]{3,2,1,0:T(8,128)(2,1)} copy(bf16[16,5,16,640]{3,0,1,2:T(8,128)(2,1)S(1)} %fusion.24) | data formatting | bytes 3276800 | tf_op jit(solution)/shard_map/convert_element_type | solution.py:123
  61.3 5.8 %all-to-all-start.1 = ((bf16[16,5,16,640]{3,2,1,0:T(8,128)(2,1)}), bf16[16,5,16,640]{3,2,1,0:T(8,128)(2,1)S(1)}, u32[]{:S(2)}, u32[]{:S(2)}) async-start(bf16[16,5,16,640]{3,2,1,0:T(8,128)(2,1)} %copy.82), calls=%async_computation.1 | async-start | bytes 3276800 | tf_op jit(solution)/shard_map/all_to_all | solution.py:122
  67.1 0.2 convert_element_type.94
  67.2 0.1 copy.79
  67.4 0.0 copy-done.3
  67.4 0.2 reshape.184
  67.6 0.0 copy-done.4
  67.6 0.0 copy-done.5
  67.7 0.0 copy-done.6
  67.7 0.1 iota_compare_fusion.8
  67.8 0.0 copy-start.7
  67.8 0.3 fusion.63
  68.0 4.7 %fusion.62 = (f32[32,4,5]{2,1,0:T(4,128)S(1)}, f32[32,4,5,128]{3,2,1,0:T(8,128)S(1)}) fusion(bf16[32,4,5,128]{3,2,1,0:T(8,128)(2,1)S(1)} %reshape.184, pred[32,128]{1,0:T(8,128)(4,1)S(1)} %iota_compare_fusion.8, bf16[32,128,512]{2,1,0:T(8,128)(2,1)} %param.21), kind=kOutput, calls=%fused_computation.85 | convolution fusion | flops 21216640 | bytes 4692480 | tf_op jit(solution)/shard_map/tgqd,tjgd->tgqj/dot_general | solution.py:37
  72.8 0.4 fusion.40
  73.3 0.1 fusion.53
  73.3 0.0 copy-done.7
  73.3 1.3 %fusion.33 = f32[32,4,5,128]{3,2,1,0:T(8,128)S(1)} fusion(f32[32,4,5,128]{3,2,1,0:T(8,128)S(1)} %get-tuple-element.7, f32[32,4,128]{2,1,0:T(4,128)S(1)} %reshape.195, f32[32,4,5]{2,1,0:T(4,128)S(1)} %get-tuple-element.5, f32[32,4,5]{2,1,0:T(4,128)S(1)} %get-tuple-element.4, f32[32,4,5]{2,1,0:T(4,128)S(1)} %multiply_maximum_fusion, ...), kind=kOutput, calls=%fused_computation.27 | convolution fusion | flops 21463040 | bytes 4926976 | tf_op jit(solution)/shard_map/tgqj,tjgd->tgqd/dot_general | solution.py:52
  74.6 0.0 copy-start.2
  74.6 0.1 reshape.188
  74.7 0.0 copy-done
  74.7 0.2 fusion.47
  74.9 0.2 select_reduce_fusion
  75.2 29.5 %all-to-all-done.1 = bf16[16,5,16,640]{3,2,1,0:T(8,128)(2,1)S(1)} async-done(((bf16[16,5,16,640]{3,2,1,0:T(8,128)(2,1)}), bf16[16,5,16,640]{3,2,1,0:T(8,128)(2,1)S(1)}, u32[]{:S(2)}, u32[]{:S(2)}) %all-to-all-start.1) | async-done | bytes 1638432 | tf_op jit(solution)/shard_map/all_to_all | solution.py:122
  104.7 0.2 bitcast_reduce_fusion
  104.9 0.5 fusion.36
  105.4 0.0 copy-done.2
  105.5 0.8 add_convert_fusion
  (11 shorter events, 0.2 us)
Async XLA Ops:
  0.6 74.1 %copy-start = (bf16[640,128]{1,0:T(8,128)(2,1)S(1)}, bf16[640,128]{1,0:T(8,128)(2,1)}, u32[]{:S(2)}) copy-start(bf16[640,128]{1,0:T(8,128)(2,1)} %param.14) | copy-start | bytes 491524
  48.9 8.5 %copy-start.1 = (bf16[16,640,640]{2,1,0:T(8,128)(2,1)S(1)}, bf16[16,640,640]{2,1,0:T(8,128)(2,1)}, u32[]{:S(2)}) copy-start(bf16[16,640,640]{2,1,0:T(8,128)(2,1)} %param.17) | copy-start | bytes 39321604
  59.7 7.7 %copy-start.3 = (bf16[32,2560]{1,0:T(8,128)(2,1)S(1)}, bf16[32,2560]{1,0:T(8,128)(2,1)}, u32[]{:S(2)}) copy-start(bf16[32,2560]{1,0:T(8,128)(2,1)} %param.18) | copy-start | bytes 491524
  59.7 7.9 %copy-start.4 = (bf16[32,512]{1,0:T(8,128)(2,1)S(1)}, bf16[32,512]{1,0:T(8,128)(2,1)}, u32[]{:S(2)}) copy-start(bf16[32,512]{1,0:T(8,128)(2,1)} %param.19) | copy-start | bytes 98308
  59.7 7.9 %copy-start.5 = (bf16[32,512]{1,0:T(8,128)(2,1)S(1)}, bf16[32,512]{1,0:T(8,128)(2,1)}, u32[]{:S(2)}) copy-start(bf16[32,512]{1,0:T(8,128)(2,1)} %param.20) | copy-start | bytes 98308
  59.8 7.9 %copy-start.6 = (s32[32]{0:T(128)S(1)}, s32[32]{0:T(128)}, u32[]{:S(2)}) copy-start(s32[32]{0:T(128)} %param.23) | copy-start | bytes 388
  61.3 43.4 %all-to-all-start.1 = ((bf16[16,5,16,640]{3,2,1,0:T(8,128)(2,1)}), bf16[16,5,16,640]{3,2,1,0:T(8,128)(2,1)S(1)}, u32[]{:S(2)}, u32[]{:S(2)}) async-start(bf16[16,5,16,640]{3,2,1,0:T(8,128)(2,1)} %copy.82), calls=%async_computation.1 | async-start | bytes 3276800 | tf_op jit(solution)/shard_map/all_to_all | solution.py:122
  67.8 5.6 %copy-start.7 = (bf16[32,128,512]{2,1,0:T(8,128)(2,1)S(1)}, bf16[32,128,512]{2,1,0:T(8,128)(2,1)}, u32[]{:S(2)}) copy-start(bf16[32,128,512]{2,1,0:T(8,128)(2,1)} %param.22) | copy-start | bytes 12582916
  74.6 30.8 %copy-start.2 = (bf16[32,2560]{1,0:T(8,128)(2,1)S(1)}, bf16[32,2560]{1,0:T(8,128)(2,1)}, u32[]{:S(2)}) copy-start(bf16[32,2560]{1,0:T(8,128)(2,1)} %param.12) | copy-start | bytes 491524
where the time goes:
time: 107 us; the launch traced here: 106 us
  blocking collectives  43.9 us (41%)
  waiting for transfers between devices  29.5 us (28%)
  matrix products  17.7 us (17%)
  local copies, waits for them, and re-layouts  6.25 us (6%)
  starting transfers between devices  5.77 us (5%)
  other arithmetic  2.19 us (2%)
    all_to_all x1, blocking collectives, per_device(): lax.all_to_all(copies, ('expert', 'mp'), split_axis=0, concat_axis=0, til...  43.9 us
    all_to_all x1, waiting for transfers between devices, per_device(): lax.all_to_all(partial_value.astype(jnp.bfloat16), ('expert', 'mp'), spli...  29.5 us
    dot_general x1, matrix products, expert_ffn(): jnp.einsum('scew,ewf->scef', received, first_weight, preferred_element_ty...  7.54 us
    all_to_all x1, starting transfers between devices, per_device(): lax.all_to_all(partial_value.astype(jnp.bfloat16), ('expert', 'mp'), spli...  5.77 us
    dot_general x1, matrix products, attend(): jnp.einsum('tgqd,tjgd->tgqj', query_heads, keys_old, preferred_element_ty...  4.73 us
    dot_general x1, matrix products, expert_ffn(): jnp.einsum('scef,efw->scew', hidden, second_weight, preferred_element_typ...  2.37 us
  transfers between devices with their start and end apart: 1, of which 1 were waited for; matrix products, arithmetic and copies ran while one was open for 7% of the time, Pallas kernels for 0%

commit v1 on v0

v1 whole, which is shorter than its diff:
```python
import functools
import math

import jax
import jax.numpy as jnp
from jax import lax
from jax.experimental import pallas as pl
from jax.experimental.pallas import tpu as pltpu
from jax.sharding import PartitionSpec as P


D = 5120
SUB = 8
HEADS = 40
HD = 128
KV_HEADS = 8
EXPERTS = 128
TOP = 2
CAP = 5


BF16 = jnp.bfloat16
F32 = jnp.float32


def log2(value):
    bits = value.bit_length() - 1
    assert value == 1 << bits
    return bits


def in_vmem(kernel, out_shape, smem=(), plain=(), hbm=(), hbm_out=(), room=6 << 20, cost=1.0, **kwargs):
    def space(i, left):
        return pl.ANY if i in left else pltpu.SMEM if i in smem else pltpu.VMEM

    def call(*args):
        specs = [pl.BlockSpec(memory_space=space(i, hbm)) for i in range(len(args))]
        args = [
            pltpu.with_memory_space_constraint(
                a, pltpu.HBM if i in smem or i in plain or i in hbm else pltpu.VMEM
            )
            for i, a in enumerate(args)
        ]
        return pl.pallas_call(
            kernel,
            out_shape=tuple(
                jax.ShapeDtypeStruct(s.shape, s.dtype) if i in hbm_out else pltpu.VMEM(s.shape, s.dtype)
                for i, s in enumerate(out_shape)
            ),
            in_specs=specs,
            out_specs=tuple(
                pl.BlockSpec(memory_space=pl.ANY if i in hbm_out else pltpu.VMEM)
                for i in range(len(out_shape))
            ),
            compiler_params=pltpu.CompilerParams(vmem_limit_bytes=room),
            cost_estimate=pl.CostEstimate(
                flops=int(cost * 5e8), bytes_accessed=int(cost * 3e6), transcendentals=0
            ),
            **kwargs,
        )(*args)

    return call


def route_kernel(
    ids_ref, res_ref, gain_ref, pos_ref, sel_ref, normed_ref, *, sub_local, per_owner, n_owner
):
    owner = lax.axis_index("expert")
    mp = lax.axis_index("mp")
    tokens = ids_ref.shape[2]
    rows = tokens * SUB
    ids = jnp.concatenate([ids_ref[s].astype(F32) for s in range(SUB)], axis=0)
    ids = jnp.concatenate([ids, jnp.zeros((EXPERTS - SUB * TOP, tokens), F32)], axis=0)
    ids = jnp.concatenate([ids, jnp.zeros((EXPERTS, EXPERTS - tokens), F32)], axis=1).T
    expert_lane = lax.broadcasted_iota(jnp.int32, (tokens, EXPERTS), 1).astype(F32)

    def hot_rows(k):
        return jnp.concatenate(
            [
                (ids[0:tokens, s * TOP + k : s * TOP + k + 1] == expert_lane).astype(F32)
                for s in range(SUB)
            ],
            axis=0,
        )

    both = jnp.concatenate([hot_rows(k) for k in range(TOP)], axis=1)
    down = lax.broadcasted_iota(jnp.int32, (rows, rows), 0)
    across = lax.broadcasted_iota(jnp.int32, (rows, rows), 1)
    earlier = (across < down).astype(F32).astype(BF16)
    before = jnp.dot(earlier, both.astype(BF16), preferred_element_type=F32)
    lane = lax.broadcasted_iota(jnp.int32, (rows, EXPERTS), 1)
    lane_f = lane.astype(F32)
    total = jnp.zeros((1, EXPERTS), F32)
    packed = jnp.zeros((rows, EXPERTS), F32)
    half = n_owner // 2
    for k in range(TOP):
        hot = both[:, k * EXPERTS : (k + 1) * EXPERTS]
        ahead = before[:, k * EXPERTS : (k + 1) * EXPERTS] + total
        total = total + jnp.sum(hot, axis=0, keepdims=True)
        slot = jnp.sum(hot * ahead, axis=1, keepdims=True).astype(jnp.int32)
        expert = jnp.sum(hot * lane_f, axis=1, keepdims=True).astype(jnp.int32)
        apart = (expert >> log2(per_owner)) ^ owner
        block = ((apart & 1) ^ mp) * half + (apart >> 1)
        flat = (block * CAP + slot) * per_owner + (expert & (per_owner - 1))
        packed = jnp.where(lane == k, flat.astype(F32), packed)
        packed = jnp.where(lane == TOP + k, expert.astype(F32), packed)
    split = sub_local * tokens
    packed = jnp.where(
        mp == 0, packed, jnp.concatenate([packed[split:], packed[:split]], axis=0)
    )
    pos_ref[...] = packed
    turned = packed.T
    slots = sel_ref.shape[0]
    slot_row = lax.broadcasted_iota(jnp.int32, (slots, rows), 0).astype(F32)
    hit = slot_row == turned[0:1, :]
    for k in range(1, TOP):
        hit = hit | (slot_row == turned[k : k + 1, :])
    sel_ref[...] = hit.astype(F32).astype(BF16)
    width = res_ref.shape[1] // sub_local
    for s, piece in enumerate(normed_rows(res_ref, gain_ref, sub_local, width)):
        normed_ref[s * tokens : (s + 1) * tokens, :] = piece


def normed_rows(res_ref, gain_ref, sub_local, width):
    out = []
    chunks = width // HD
    for s in range(sub_local):
        piece = res_ref[:, s * width : (s + 1) * width].astype(F32)
        meansq = jnp.mean(piece * piece, axis=-1, keepdims=True)
        scaled = piece * lax.rsqrt(meansq + 1e-06)
        gained = [
            scaled[:, c * HD : (c + 1) * HD]
            * gain_ref[s * chunks + c : s * chunks + c + 1, :].astype(F32)
            for c in range(chunks)
        ]
        out.append(jnp.concatenate(gained, axis=1).astype(BF16))
    return out


def dispatch_kernel(normed_ref, peer_ref, peer_gain_ref, sel_ref, *out_refs, sub_local, width):
    rows = normed_rows(peer_ref, peer_gain_ref, sub_local, width)
    normed = jnp.concatenate([normed_ref[...]] + rows, axis=0)
    sent = jnp.dot(sel_ref[...], normed, preferred_element_type=F32).astype(BF16)
    slots = out_refs[0].shape[0]
    for j, ref in enumerate(out_refs):
        ref[...] = sent[j * slots : (j + 1) * slots]


def gate(normed, router, pos_ref, out_ref):
    logits = jnp.dot(normed, router, preferred_element_type=F32)
    rows = normed.shape[0]
    lane = lax.broadcasted_iota(jnp.int32, (rows, EXPERTS), 1)
    scores = []
    for k in range(TOP):
        expert = pos_ref[0:rows, TOP + k : TOP + k + 1].astype(jnp.int32)
        picked = jnp.sum(jnp.where(lane == expert, logits, 0.0), axis=1, keepdims=True)
        scores.append(jax.nn.sigmoid(picked))
    total = functools.reduce(lambda a, b: a + b, scores)
    out = jnp.zeros((rows, EXPERTS), F32)
    for k in range(TOP):
        out = jnp.where(lane == k, scores[k] / total, out)
    out_ref[...] = out


def combine_kernel(pos_ref, weight_ref, res_ref, context_ref, *refs, sub_local, width):
    blocks, out_ref = refs[:-1], refs[-1]
    tokens = res_ref.shape[0]
    rows = sub_local * tokens
    returned = jnp.concatenate([ref[...] for ref in blocks], axis=0)
    slots = returned.shape[0]
    lane = lax.broadcasted_iota(jnp.int32, (rows, slots), 1)
    moe = jnp.zeros((rows, width), F32)
    for k in range(TOP):
        flat = pos_ref[0:rows, k : k + 1].astype(jnp.int32)
        hot = (lane == flat).astype(F32).astype(BF16)
        picked = jnp.dot(hot, returned, preferred_element_type=F32)
        moe = moe + weight_ref[:, k : k + 1] * picked
    for s in range(sub_local):
        at = slice(s * width, (s + 1) * width)
        total = res_ref[:, at].astype(F32) + context_ref[:, at]
        out_ref[:, at] = (total + moe[s * tokens : (s + 1) * tokens]).astype(BF16)


def attend_kernel(
    length_ref,
    query_ref,
    key_ref,
    value_ref,
    cache_key_ref,
    cache_value_ref,
    normed_ref,
    router_ref,
    pos_ref,
    attention_ref,
    context_ref,
    gate_ref,
    spread_ref,
    gather_ref,
    new_key_ref,
    new_value_ref,
    rounded_ref,
    store_sem,
):
    tokens = query_ref.shape[0]
    unroll = math.gcd(tokens, 16)
    groups = key_ref.shape[1] // HD
    per_group = HEADS // KV_HEADS
    heads = groups * per_group
    pad = spread_ref.shape[0] // tokens
    cache_len = cache_key_ref.shape[1]
    scale = 1.0 / math.sqrt(HD)
    new_key_ref[...] = key_ref[...].astype(F32)
    new_value_ref[...] = value_ref[...].astype(F32)
    for h in range(heads, pad):
        spread_ref[pl.ds(h, tokens, stride=pad), :] = jnp.zeros((tokens, HD), F32)
    for h in range(heads):
        spread_ref[pl.ds(h, tokens, stride=pad), :] = query_ref[:, h * HD : (h + 1) * HD].astype(F32)
    lane = lax.broadcasted_iota(jnp.int32, (pad, cache_len), 1)
    row = lax.broadcasted_iota(jnp.int32, (pad, HD), 0)
    lane = lax.broadcasted_iota(jnp.int32, (pad, cache_len), 1)
    member = [(row >= g * per_group) & (row < (g + 1) * per_group) for g in range(groups)]

    def by_group(x):
        out = jnp.broadcast_to(x[:, 0:HD], (pad, HD))
        for g in range(1, groups):
            out = jnp.where(member[g], x[:, g * HD : (g + 1) * HD], out)
        return out

    for i in range(tokens // unroll):
        at = slice(i * unroll * pad, (i + 1) * unroll * pad)
        inner = [i * unroll + u for u in range(unroll)]
        queries = spread_ref[at, :]
        scores = []
        for u, t in enumerate(inner):
            own = queries[u * pad : (u + 1) * pad]
            query = jnp.concatenate([jnp.where(one, own, 0.0) for one in member], axis=1)
            scores.append(
                lax.dot_general(
                    query.astype(BF16),
                    cache_key_ref[t],
                    (((1,), (1,)), ((), ())),
                    preferred_element_type=F32,
                )
            )
        usable = jnp.concatenate([lane < length_ref[t] for t in inner], axis=0)
        scores = jnp.where(usable, jnp.concatenate(scores, axis=0) * scale, -1e30)
        new_key = jnp.concatenate([by_group(new_key_ref[t : t + 1, :]) for t in inner], axis=0)
        new_value = jnp.concatenate([by_group(new_value_ref[t : t + 1, :]) for t in inner], axis=0)
        fresh = jnp.sum(queries * new_key, axis=1, keepdims=True) * scale
        row_max = jnp.maximum(jnp.max(scores, axis=1, keepdims=True), fresh)
        expo = jnp.where(usable, jnp.exp(scores - row_max), 0.0)
        expo_new = jnp.exp(fresh - row_max)
        total = jnp.sum(expo, axis=1, keepdims=True) + expo_new
        probs = expo / total
        prob_new = (expo_new / total).astype(BF16).astype(F32)
        context = [
            by_group(
                jnp.dot(
                    probs[u * pad : (u + 1) * pad].astype(BF16),
                    cache_value_ref[t],
                    preferred_element_type=F32,
                )
            )
            for u, t in enumerate(inner)
        ]
        gather_ref[at, :] = jnp.concatenate(context, axis=0) + prob_new * new_value
    for h in range(heads):
        context = gather_ref[pl.ds(h, tokens, stride=pad), :]
        context_ref[:, h * HD : (h + 1) * HD] = context
        rounded_ref[:, h * HD : (h + 1) * HD] = context.astype(BF16)
    store = pltpu.make_async_copy(rounded_ref, attention_ref, store_sem)
    store.start()
    gate(normed_ref[...], router_ref[...], pos_ref, gate_ref)
    store.wait()


def ffn_kernel(*refs, n_block, per_owner):
    blocks = refs[:n_block]
    first_ref, second_ref, mine_ref, other_ref, rows_ref, out_ref = refs[n_block:]
    slots, width = blocks[0].shape
    lanes = range(width // HD)
    for b in range(n_block):
        block = blocks[b][...].astype(F32)
        for c in lanes:
            rows_ref[c, b * slots : (b + 1) * slots, :] = block[:, c * HD : (c + 1) * HD]
    depth = n_block * slots // per_owner
    at = [pl.ds(e, depth, stride=per_owner) for e in range(per_owner)]
    taken = [
        jnp.concatenate([rows_ref[c, a, :] for c in lanes], axis=1).astype(BF16) for a in at
    ]
    hidden = [
        jnp.dot(x, first_ref[e], preferred_element_type=F32) for e, x in enumerate(taken)
    ]
    hidden = [jax.nn.gelu(h).astype(BF16) for h in hidden]
    for e, h in enumerate(hidden):
        result = jnp.dot(h, second_ref[e], preferred_element_type=F32)
        for c in lanes:
            out_ref[c, at[e], :] = result[:, c * HD : (c + 1) * HD]
    split = n_block // 2 * slots
    for c in lanes:
        mine_ref[:, c * HD : (c + 1) * HD] = out_ref[c, 0:split, :]
        other_ref[:, c * HD : (c + 1) * HD] = out_ref[c, split : 2 * split, :].astype(BF16)


def reduce_kernel(mine_ref, other_ref, *out_refs):
    slots = out_refs[0].shape[0]
    for j, ref in enumerate(out_refs):
        at = slice(j * slots, (j + 1) * slots)
        ref[...] = (mine_ref[at, :] + other_ref[at, :].astype(F32)).astype(BF16)


def per_device(
    residual,
    norm_gain,
    router_weight,
    expert_ids,
    expert_in,
    expert_out,
    queries,
    new_keys,
    new_values,
    cache_keys,
    cache_values,
    lengths,
):
    width = D // SUB
    tokens = residual.shape[0]
    sub_local = residual.shape[1] // width
    n_owner = lax.axis_size("expert")
    n_mp = lax.axis_size("mp")
    assert n_mp == 2
    per_owner = expert_in.shape[0]
    slots = CAP * per_owner
    half = n_owner // 2
    rows = tokens * SUB
    gain = norm_gain.reshape(-1, HD)

    swap = [(0, 1), (1, 0)]
    order = sorted(range(half), key=lambda j: (-j.bit_length(), j))

    def partners(j):
        return [
            (e * n_mp + m, (e ^ (2 * j + m)) * n_mp + m) for e in range(n_owner) for m in range(n_mp)
        ]

    peer_residual = lax.ppermute(residual, "mp", swap)
    peer_gain = lax.ppermute(gain, "mp", swap)
    pos, sel, normed = in_vmem(
        functools.partial(route_kernel, sub_local=sub_local, per_owner=per_owner, n_owner=n_owner),
        (
            jax.ShapeDtypeStruct((rows, EXPERTS), F32),
            jax.ShapeDtypeStruct((half * slots, rows), BF16),
            jax.ShapeDtypeStruct((sub_local * tokens, width), BF16),
        ),
        plain=(0, 1, 2),
        cost=20.0,
        name="route",
    )(expert_ids.transpose(1, 2, 0), residual, gain)
    sent = in_vmem(
        functools.partial(dispatch_kernel, sub_local=sub_local, width=width),
        tuple(jax.ShapeDtypeStruct((slots, width), BF16) for _ in range(half)),
        cost=20.0,
        name="dispatch",
    )(normed, peer_residual, peer_gain, sel)

    own = [None] * half
    for j in order:
        own[j] = lax.ppermute(sent[j], ("expert", "mp"), partners(j))
    groups = new_keys.shape[1] // HD
    pad = -(-groups * (HEADS // KV_HEADS) // 8) * 8
    attention, context, weights = in_vmem(
        attend_kernel,
        (
            jax.ShapeDtypeStruct(queries.shape, BF16),
            jax.ShapeDtypeStruct(queries.shape, F32),
            jax.ShapeDtypeStruct((sub_local * tokens, EXPERTS), F32),
        ),
        smem=(0,),
        hbm_out=(0,),
        scratch_shapes=(
            pltpu.VMEM((tokens * pad, HD), F32),
            pltpu.VMEM((tokens * pad, HD), F32),
            pltpu.VMEM(new_keys.shape, F32),
            pltpu.VMEM(new_values.shape, F32),
            pltpu.VMEM(queries.shape, BF16),
            pltpu.SemaphoreType.DMA,
        ),
        cost=4.0,
        name="attend",
    )(
        lengths,
        queries,
        new_keys,
        new_values,
        cache_keys,
        cache_values,
        normed,
        router_weight,
        pos,
    )
    peer = [lax.ppermute(block, "mp", swap) for block in own]

    mine, other = in_vmem(
        functools.partial(ffn_kernel, n_block=n_owner, per_owner=per_owner),
        (
            jax.ShapeDtypeStruct((half * slots, width), F32),
            jax.ShapeDtypeStruct((half * slots, width), BF16),
        ),
        scratch_shapes=(
            pltpu.VMEM((width // HD, n_owner * slots, HD), F32),
            pltpu.VMEM((width // HD, n_owner * slots, HD), F32),
        ),
        room=12 << 20,
        cost=5.0,
        name="ffn",
    )(*own, *peer, expert_in, expert_out)
    result = in_vmem(
        reduce_kernel,
        tuple(jax.ShapeDtypeStruct((slots, width), BF16) for _ in range(half)),
        name="reduce",
    )(mine, lax.ppermute(other, "mp", swap))

    back = [None] * half
    for j in order:
        back[j] = lax.ppermute(result[j], ("expert", "mp"), partners(j))
    peer_back = [lax.ppermute(block, "mp", swap) for block in back]
    (mixed,) = in_vmem(
        functools.partial(combine_kernel, sub_local=sub_local, width=width),
        (jax.ShapeDtypeStruct(residual.shape, BF16),),
        name="combine",
    )(pos, weights, residual, context, *back, *peer_back)
    return (attention, mixed)


def solution(mesh):
    placed = (
        P(("groups", "expert"), "mp"),
        P("mp"),
        P(),
        P(("groups", "expert"), None, None),
        P("expert", None, "mp"),
        P("expert", "mp", None),
        P(("groups", "expert"), "mp"),
        P(("groups", "expert"), "mp"),
        P(("groups", "expert"), "mp"),
        P(("groups", "expert"), None, "mp"),
        P(("groups", "expert"), None, "mp"),
        P(("groups", "expert")),
    )
    return jax.shard_map(
        per_device,
        mesh=mesh,
        in_specs=placed,
        out_specs=(P(("groups", "expert"), "mp"), P(("groups", "expert"), "mp")),
        check_vma=False,
    )
```

time: 107 us -> 47.2 us (0.44)
  the two profiles are of different devices: /device:TPU:13 before, /device:TPU:0 now
where the time goes in v1:
time: 47.2 us; the launch traced here: 47 us
  starting transfers between devices  30.3 us (64%)
  Pallas kernels  10.9 us (23%)
  waiting for transfers between devices  4.15 us (9%)
  between operations  0.94 us (2%)
  local copies, waits for them, and re-layouts  0.74 us (2%)
    pallas_call x6, Pallas kernels, call(): pl.pallas_call(kernel, out_shape=tuple((jax.ShapeDtypeStruct(s.shape, s.d...  10.9 us
    ppermute x4, starting transfers between devices, per_device(): peer = [lax.ppermute(block, 'mp', swap) for block in own]  9.83 us
    ppermute x4, starting transfers between devices, per_device(): peer_back = [lax.ppermute(block, 'mp', swap) for block in back]  7.94 us
    ppermute x4, starting transfers between devices, per_device(): own[j] = lax.ppermute(sent[j], ('expert', 'mp'), partners(j))  6.52 us
    ppermute x4, starting transfers between devices, per_device(): back[j] = lax.ppermute(result[j], ('expert', 'mp'), partners(j))  5.12 us
    ppermute x1, waiting for transfers between devices, per_device(): lax.ppermute(other, 'mp', swap)  1.6 us
    ppermute x4, waiting for transfers between devices, per_device(): peer = [lax.ppermute(block, 'mp', swap) for block in own]  1.29 us
    ppermute x4, waiting for transfers between devices, per_device(): back[j] = lax.ppermute(result[j], ('expert', 'mp'), partners(j))  1.24 us
  transfers between devices with their start and end apart: 19, of which 4 were waited for; matrix products, arithmetic and copies ran while one was open for 0% of the time, Pallas kernels for 11%

profile of v1, /device:TPU:0, one launch (start us, length us, event | category | flops | bytes accessed | tf_op | source)
XLA Modules:
  0.0 47.0 jit_solution(14471821943163668006)
XLA Ops:
  0.6 0.6 %collective-permute-start.1 = (bf16[20,128]{1,0:T(8,128)(2,1)}, bf16[20,128]{1,0:T(8,128)(2,1)S(1)}, u32[]{:S(2)}, u32[]{:S(2)}) collective-permute-start(bf16[20,128]{1,0:T(8,128)(2,1)} %bitcast.7), channel_id=1, source_target_pairs={{0,1},{1,0},{2,3},{3,2},{4,5},{5,4},{6,7},{7,6},{8,9},{9,8},{10,11... | collective-permute-start | bytes 15368 | tf_op jit(solution)/shard_map/ppermute | solution.py:347
  1.2 0.1 collective-permute-start
  1.3 1.7 %route.1 = (f32[256,128]{1,0:T(8,128)S(1)}, bf16[320,256]{1,0:T(8,128)(2,1)S(1)}, bf16[128,640]{1,0:T(8,128)(2,1)S(1)}) custom-call(s32[8,2,32]{2,1,0:T(2,128)} %bitcast.6, bf16[32,2560]{1,0:T(8,128)(2,1)} %res_ref.3, bf16[20,128]{1,0:T(8,128)(2,1)} %bitcast.8), custom_call_target="tpu_custom_call" | custom-call | flops 10000000000 | bytes 60000000 | tf_op jit(solution)/shard_map/route/pallas_call | solution.py:44
  3.0 0.0 collective-permute-done.1.peer_gain_ref
  3.0 0.0 collective-permute-done.peer_ref
  3.0 0.0 slice-start.2
  3.0 0.0 slice-start.3
  3.0 0.0 slice-start.6
  3.1 0.0 slice-start.7
  3.1 0.4 dispatch.1
  3.4 0.8 %collective-permute-start.2 = (bf16[80,640]{1,0:T(8,128)(2,1)S(1)}, bf16[80,640]{1,0:T(8,128)(2,1)S(1)}, u32[]{:S(2)}, u32[]{:S(2)}) collective-permute-start(bf16[80,640]{1,0:T(8,128)(2,1)S(1)} %get-tuple-element.24), channel_id=1, source_target_pairs={{0,0},{1,3},{2,2},{3,1},{4,4},{5,7},{6,6},{7,5},{8,8},{9,11},{10,1... | collective-permute-start | bytes 307208 | tf_op jit(solution)/shard_map/ppermute | solution.py:368
  4.3 3.1 %collective-permute-start.3 = (bf16[80,640]{1,0:T(8,128)(2,1)S(1)}, bf16[80,640]{1,0:T(8,128)(2,1)S(1)}, u32[]{:S(2)}, u32[]{:S(2)}) collective-permute-start(bf16[80,640]{1,0:T(8,128)(2,1)S(1)} %get-tuple-element.25), channel_id=1, source_target_pairs={{0,4},{1,7},{2,6},{3,5},{4,0},{5,3},{6,2},{7,1},{8,12},{9,15},{10,... | collective-permute-start | bytes 307208 | tf_op jit(solution)/shard_map/ppermute | solution.py:368
  7.3 2.6 %collective-permute-start.4 = (bf16[80,640]{1,0:T(8,128)(2,1)S(1)}, bf16[80,640]{1,0:T(8,128)(2,1)S(1)}, u32[]{:S(2)}, u32[]{:S(2)}) collective-permute-start(bf16[80,640]{1,0:T(8,128)(2,1)S(1)} %get-tuple-element.26), channel_id=1, source_target_pairs={{0,8},{1,11},{2,10},{3,9},{4,12},{5,15},{6,14},{7,13},{8,0},{9,3},... | collective-permute-start | bytes 307208 | tf_op jit(solution)/shard_map/ppermute | solution.py:368
  9.9 0.0 copy-start.4
  9.9 0.0 copy-start.5
  9.9 0.0 copy-start.6
  10.0 0.1 collective-permute-start.5
  10.0 0.0 collective-permute-done.2.refs_0_
  10.0 3.2 %collective-permute-start.6 = (bf16[80,640]{1,0:T(8,128)(2,1)S(1)}, bf16[80,640]{1,0:T(8,128)(2,1)S(1)}, u32[]{:S(2)}, u32[]{:S(2)}) collective-permute-start(bf16[80,640]{1,0:T(8,128)(2,1)S(1)} %collective-permute-done.2.refs_0_), channel_id=1, source_target_pairs={{0,1},{1,0},{2,3},{3,2},{4,5},{5,4},{6,7},{7,6},{8,9},{9,8},{10,11... | collective-permute-start | bytes 307208 | tf_op jit(solution)/shard_map/ppermute | solution.py:401
  13.3 0.0 collective-permute-done.3.refs_1_
  13.3 0.7 %collective-permute-start.7 = (bf16[80,640]{1,0:T(8,128)(2,1)S(1)}, bf16[80,640]{1,0:T(8,128)(2,1)S(1)}, u32[]{:S(2)}, u32[]{:S(2)}) collective-permute-start(bf16[80,640]{1,0:T(8,128)(2,1)S(1)} %collective-permute-done.3.refs_1_), channel_id=1, source_target_pairs={{0,1},{1,0},{2,3},{3,2},{4,5},{5,4},{6,7},{7,6},{8,9},{9,8},{10,11... | collective-permute-start | bytes 307208 | tf_op jit(solution)/shard_map/ppermute | solution.py:401
  14.0 0.0 collective-permute-done.4.refs_2_
  14.0 5.9 %collective-permute-start.8 = (bf16[80,640]{1,0:T(8,128)(2,1)S(1)}, bf16[80,640]{1,0:T(8,128)(2,1)S(1)}, u32[]{:S(2)}, u32[]{:S(2)}) collective-permute-start(bf16[80,640]{1,0:T(8,128)(2,1)S(1)} %collective-permute-done.4.refs_2_), channel_id=1, source_target_pairs={{0,1},{1,0},{2,3},{3,2},{4,5},{5,4},{6,7},{7,6},{8,9},{9,8},{10,11... | collective-permute-start | bytes 307208 | tf_op jit(solution)/shard_map/ppermute | solution.py:401
  19.9 0.0 collective-permute-done.5.refs_3_
  19.9 0.0 collective-permute-start.9
  19.9 0.0 collective-permute-done.6.refs_4_
  19.9 0.0 collective-permute-done.7.refs_5_
  19.9 0.9 %collective-permute-done.8.refs_6_ = bf16[80,640]{1,0:T(8,128)(2,1)S(1)} collective-permute-done((bf16[80,640]{1,0:T(8,128)(2,1)S(1)}, bf16[80,640]{1,0:T(8,128)(2,1)S(1)}, u32[]{:S(2)}, u32[]{:S(2)}) %collective-permute-start.8) | collective-permute-done | bytes 102432 | tf_op jit(solution)/shard_map/ppermute | solution.py:401
  20.8 0.4 collective-permute-done.9.refs_7_
  21.2 0.0 slice-done
  21.2 0.0 slice-done.1
  21.2 0.0 slice-done.4
  21.2 0.0 slice-done.5
  21.2 0.0 slice-done.2
  21.2 0.0 slice-done.3
  21.2 0.0 slice-done.6
  21.2 0.0 slice-done.7
  21.3 4.6 %ffn.1 = (f32[320,640]{1,0:T(8,128)S(1)}, bf16[320,640]{1,0:T(8,128)(2,1)S(1)}) custom-call(bf16[80,640]{1,0:T(8,128)(2,1)S(1)} %collective-permute-done.2.refs_0_, bf16[80,640]{1,0:T(8,128)(2,1)S(1)} %collective-permute-done.3.refs_1_, bf16[80,640]{1,0:T(8,128)(2,1)S(1)} %collective-permute-done.4.refs_2_, ...), custom_call_target="tpu_custom_call" | custom-call | flops 2500000000 | bytes 15000000 | tf_op jit(solution)/shard_map/ffn/pallas_call | solution.py:44
  25.9 0.2 collective-permute-start.10
  26.1 1.6 %collective-permute-done.10.other_ref = bf16[320,640]{1,0:T(8,128)(2,1)S(1)} collective-permute-done((bf16[320,640]{1,0:T(8,128)(2,1)S(1)}, bf16[320,640]{1,0:T(8,128)(2,1)S(1)}, u32[]{:S(2)}, u32[]{:S(2)}) %collective-permute-start.10) | collective-permute-done | bytes 409632 | tf_op jit(solution)/shard_map/ppermute | solution.py:421
  27.7 0.1 reduce.1
  27.8 0.7 %collective-permute-start.11 = (bf16[80,640]{1,0:T(8,128)(2,1)S(1)}, bf16[80,640]{1,0:T(8,128)(2,1)S(1)}, u32[]{:S(2)}, u32[]{:S(2)}) collective-permute-start(bf16[80,640]{1,0:T(8,128)(2,1)S(1)} %get-tuple-element.30), channel_id=1, source_target_pairs={{0,0},{1,3},{2,2},{3,1},{4,4},{5,7},{6,6},{7,5},{8,8},{9,11},{10,1... | collective-permute-start | bytes 307208 | tf_op jit(solution)/shard_map/ppermute | solution.py:425
  28.5 1.7 %collective-permute-start.12 = (bf16[80,640]{1,0:T(8,128)(2,1)S(1)}, bf16[80,640]{1,0:T(8,128)(2,1)S(1)}, u32[]{:S(2)}, u32[]{:S(2)}) collective-permute-start(bf16[80,640]{1,0:T(8,128)(2,1)S(1)} %get-tuple-element.31), channel_id=1, source_target_pairs={{0,4},{1,7},{2,6},{3,5},{4,0},{5,3},{6,2},{7,1},{8,12},{9,15},{10,... | collective-permute-start | bytes 307208 | tf_op jit(solution)/shard_map/ppermute | solution.py:425
  30.2 1.7 %collective-permute-start.13 = (bf16[80,640]{1,0:T(8,128)(2,1)S(1)}, bf16[80,640]{1,0:T(8,128)(2,1)S(1)}, u32[]{:S(2)}, u32[]{:S(2)}) collective-permute-start(bf16[80,640]{1,0:T(8,128)(2,1)S(1)} %get-tuple-element.32), channel_id=1, source_target_pairs={{0,8},{1,11},{2,10},{3,9},{4,12},{5,15},{6,14},{7,13},{8,0},{9,3},... | collective-permute-start | bytes 307208 | tf_op jit(solution)/shard_map/ppermute | solution.py:425
  31.9 1.0 %collective-permute-start.14 = (bf16[80,640]{1,0:T(8,128)(2,1)S(1)}, bf16[80,640]{1,0:T(8,128)(2,1)S(1)}, u32[]{:S(2)}, u32[]{:S(2)}) collective-permute-start(bf16[80,640]{1,0:T(8,128)(2,1)S(1)} %get-tuple-element.33), channel_id=1, source_target_pairs={{0,12},{1,15},{2,14},{3,13},{4,8},{5,11},{6,10},{7,9},{8,4},{9,7},... | collective-permute-start | bytes 307208 | tf_op jit(solution)/shard_map/ppermute | solution.py:425
  32.9 0.0 collective-permute-done.11.refs_0_
  32.9 2.6 %collective-permute-start.15 = (bf16[80,640]{1,0:T(8,128)(2,1)S(1)}, bf16[80,640]{1,0:T(8,128)(2,1)S(1)}, u32[]{:S(2)}, u32[]{:S(2)}) collective-permute-start(bf16[80,640]{1,0:T(8,128)(2,1)S(1)} %collective-permute-done.11.refs_0_), channel_id=1, source_target_pairs={{0,1},{1,0},{2,3},{3,2},{4,5},{5,4},{6,7},{7,6},{8,9},{9,8},{10,11... | collective-permute-start | bytes 307208 | tf_op jit(solution)/shard_map/ppermute | solution.py:426
  35.6 0.0 collective-permute-done.12.refs_1_
  35.6 0.4 collective-permute-start.16
  36.0 1.2 %collective-permute-done.13.refs_2_ = bf16[80,640]{1,0:T(8,128)(2,1)S(1)} collective-permute-done((bf16[80,640]{1,0:T(8,128)(2,1)S(1)}, bf16[80,640]{1,0:T(8,128)(2,1)S(1)}, u32[]{:S(2)}, u32[]{:S(2)}) %collective-permute-start.13) | collective-permute-done | bytes 102432 | tf_op jit(solution)/shard_map/ppermute | solution.py:425
  37.2 4.9 %collective-permute-start.17 = (bf16[80,640]{1,0:T(8,128)(2,1)S(1)}, bf16[80,640]{1,0:T(8,128)(2,1)S(1)}, u32[]{:S(2)}, u32[]{:S(2)}) collective-permute-start(bf16[80,640]{1,0:T(8,128)(2,1)S(1)} %collective-permute-done.13.refs_2_), channel_id=1, source_target_pairs={{0,1},{1,0},{2,3},{3,2},{4,5},{5,4},{6,7},{7,6},{8,9},{9,8},{10,11... | collective-permute-start | bytes 307208 | tf_op jit(solution)/shard_map/ppermute | solution.py:426
  42.1 0.0 collective-permute-done.14.refs_3_
  42.1 0.0 collective-permute-start.18
  42.1 0.0 copy-done
  42.1 0.0 copy-done.1
  42.1 0.0 copy-done.2
  42.2 3.5 %attend.1 = (bf16[32,2560]{1,0:T(8,128)(2,1)}, f32[32,2560]{1,0:T(8,128)S(1)}, f32[128,128]{1,0:T(8,128)S(1)}) custom-call(s32[32]{0:T(128)} %length_ref.1, bf16[32,2560]{1,0:T(8,128)(2,1)S(1)} %copy-done.2, bf16[32,512]{1,0:T(8,128)(2,1)S(1)} %copy-done.4, bf16[32,512]{1,0:T(8,128)(2,1)S(1)} %copy-done.5, bf16[32,128,512]{2,1,0:T(8,128)(2,1)S(1)} %copy-done, ...), custom_call_target="tpu_custom_call" | custom-call | flops 2000000000 | bytes 12000000 | tf_op jit(solution)/shard_map/attend/pallas_call | solution.py:44
  45.7 0.0 collective-permute-done.15.refs_4_
  45.7 0.0 collective-permute-done.16.refs_5_
  45.7 0.0 collective-permute-done.17.refs_6_
  45.7 0.0 collective-permute-done.18.refs_7_
  45.8 0.0 copy-done.6
  45.8 0.5 %combine.1 = bf16[32,2560]{1,0:T(8,128)(2,1)S(1)} custom-call(f32[256,128]{1,0:T(8,128)S(1)} %get-tuple-element.19.pos_ref, f32[128,128]{1,0:T(8,128)S(1)} %get-tuple-element.21.weight_ref, bf16[32,2560]{1,0:T(8,128)(2,1)S(1)} %copy-done.6, f32[32,2560]{1,0:T(8,128)S(1)} %get-tuple-element.22.context_ref, ...), custom_call_target="tpu_custom_call" | custom-call | flops 500000000 | bytes 3000000 | tf_op jit(solution)/shard_map/combine/pallas_call | solution.py:44
  46.3 0.7 %copy.14 = bf16[32,2560]{1,0:T(8,128)(2,1)} copy(bf16[32,2560]{1,0:T(8,128)(2,1)S(1)} %combine.1) | data formatting | bytes 327680
  (13 shorter events, 0.0 us)
Async XLA Ops:
  0.6 2.4 %collective-permute-start.1 = (bf16[20,128]{1,0:T(8,128)(2,1)}, bf16[20,128]{1,0:T(8,128)(2,1)S(1)}, u32[]{:S(2)}, u32[]{:S(2)}) collective-permute-start(bf16[20,128]{1,0:T(8,128)(2,1)} %bitcast.7), channel_id=1, source_target_pairs={{0,1},{1,0},{2,3},{3,2},{4,5},{5,4},{6,7},{7,6},{8,9},{9,8},{10,11... | collective-permute-start | bytes 15368 | tf_op jit(solution)/shard_map/ppermute | solution.py:347
  1.2 1.8 %collective-permute-start = (bf16[32,2560]{1,0:T(8,128)(2,1)}, bf16[32,2560]{1,0:T(8,128)(2,1)S(1)}, u32[]{:S(2)}, u32[]{:S(2)}) collective-permute-start(bf16[32,2560]{1,0:T(8,128)(2,1)} %res_ref.3), channel_id=1, source_target_pairs={{0,1},{1,0},{2,3},{3,2},{4,5},{5,4},{6,7},{7,6},{8,9},{9,8},{10,11... | collective-permute-start | bytes 491528 | tf_op jit(solution)/shard_map/ppermute | solution.py:346
  1.3 19.9 %slice-start = ((s8[13107200]{0:T(1024)(128)(4,1)}), s8[4194304]{0:T(1024)(128)(4,1)S(1)}, s32[]{:S(2)}) async-start(s8[13107200]{0:T(1024)(128)(4,1)} %bitcast.2), calls=%async_computation | async-start | bytes 8388608
  1.3 19.9 %slice-start.1 = ((s8[13107200]{0:T(1024)(128)(4,1)}), s8[4194304]{0:T(1024)(128)(4,1)S(1)}, s32[]{:S(2)}) async-start(s8[13107200]{0:T(1024)(128)(4,1)} %bitcast.2), calls=%async_computation.1 | async-start | bytes 8388608
  1.3 19.9 %slice-start.4 = ((s8[13107200]{0:T(1024)(128)(4,1)}), s8[4194304]{0:T(1024)(128)(4,1)S(1)}, s32[]{:S(2)}) async-start(s8[13107200]{0:T(1024)(128)(4,1)} %bitcast.4), calls=%async_computation.4 | async-start | bytes 8388608
  1.3 19.9 %slice-start.5 = ((s8[13107200]{0:T(1024)(128)(4,1)}), s8[4194304]{0:T(1024)(128)(4,1)S(1)}, s32[]{:S(2)}) async-start(s8[13107200]{0:T(1024)(128)(4,1)} %bitcast.4), calls=%async_computation.5 | async-start | bytes 8388608
  3.0 18.2 %slice-start.2 = ((s8[13107200]{0:T(1024)(128)(4,1)}), s8[4194304]{0:T(1024)(128)(4,1)S(1)}, s32[]{:S(2)}) async-start(s8[13107200]{0:T(1024)(128)(4,1)} %bitcast.2), calls=%async_computation.2 | async-start | bytes 8388608
  3.0 18.2 %slice-start.3 = ((s8[13107200]{0:T(1024)(128)(4,1)}), s8[524288]{0:T(1024)(128)(4,1)S(1)}, s32[]{:S(2)}) async-start(s8[13107200]{0:T(1024)(128)(4,1)} %bitcast.2), calls=%async_computation.3 | async-start | bytes 1048576
  3.0 18.2 %slice-start.6 = ((s8[13107200]{0:T(1024)(128)(4,1)}), s8[4194304]{0:T(1024)(128)(4,1)S(1)}, s32[]{:S(2)}) async-start(s8[13107200]{0:T(1024)(128)(4,1)} %bitcast.4), calls=%async_computation.6 | async-start | bytes 8388608
  3.1 18.2 %slice-start.7 = ((s8[13107200]{0:T(1024)(128)(4,1)}), s8[524288]{0:T(1024)(128)(4,1)S(1)}, s32[]{:S(2)}) async-start(s8[13107200]{0:T(1024)(128)(4,1)} %bitcast.4), calls=%async_computation.7 | async-start | bytes 1048576
  3.4 6.6 %collective-permute-start.2 = (bf16[80,640]{1,0:T(8,128)(2,1)S(1)}, bf16[80,640]{1,0:T(8,128)(2,1)S(1)}, u32[]{:S(2)}, u32[]{:S(2)}) collective-permute-start(bf16[80,640]{1,0:T(8,128)(2,1)S(1)} %get-tuple-element.24), channel_id=1, source_target_pairs={{0,0},{1,3},{2,2},{3,1},{4,4},{5,7},{6,6},{7,5},{8,8},{9,11},{10,1... | collective-permute-start | bytes 307208 | tf_op jit(solution)/shard_map/ppermute | solution.py:368
  4.3 9.0 %collective-permute-start.3 = (bf16[80,640]{1,0:T(8,128)(2,1)S(1)}, bf16[80,640]{1,0:T(8,128)(2,1)S(1)}, u32[]{:S(2)}, u32[]{:S(2)}) collective-permute-start(bf16[80,640]{1,0:T(8,128)(2,1)S(1)} %get-tuple-element.25), channel_id=1, source_target_pairs={{0,4},{1,7},{2,6},{3,5},{4,0},{5,3},{6,2},{7,1},{8,12},{9,15},{10,... | collective-permute-start | bytes 307208 | tf_op jit(solution)/shard_map/ppermute | solution.py:368
  7.3 6.7 %collective-permute-start.4 = (bf16[80,640]{1,0:T(8,128)(2,1)S(1)}, bf16[80,640]{1,0:T(8,128)(2,1)S(1)}, u32[]{:S(2)}, u32[]{:S(2)}) collective-permute-start(bf16[80,640]{1,0:T(8,128)(2,1)S(1)} %get-tuple-element.26), channel_id=1, source_target_pairs={{0,8},{1,11},{2,10},{3,9},{4,12},{5,15},{6,14},{7,13},{8,0},{9,3},... | collective-permute-start | bytes 307208 | tf_op jit(solution)/shard_map/ppermute | solution.py:368
  9.9 32.2 %copy-start = (bf16[32,128,512]{2,1,0:T(8,128)(2,1)S(1)}, bf16[32,128,512]{2,1,0:T(8,128)(2,1)}, u32[]{:S(2)}) copy-start(bf16[32,128,512]{2,1,0:T(8,128)(2,1)} %cache_key_ref.1) | copy-start | bytes 12582916
  9.9 32.2 %copy-start.1 = (bf16[32,128,512]{2,1,0:T(8,128)(2,1)S(1)}, bf16[32,128,512]{2,1,0:T(8,128)(2,1)}, u32[]{:S(2)}) copy-start(bf16[32,128,512]{2,1,0:T(8,128)(2,1)} %cache_value_ref.1) | copy-start | bytes 12582916
  9.9 32.2 %copy-start.2 = (bf16[32,2560]{1,0:T(8,128)(2,1)S(1)}, bf16[32,2560]{1,0:T(8,128)(2,1)}, u32[]{:S(2)}) copy-start(bf16[32,2560]{1,0:T(8,128)(2,1)} %query_ref.1) | copy-start | bytes 491524
  9.9 32.2 %copy-start.3 = (bf16[640,128]{1,0:T(8,128)(2,1)S(1)}, bf16[640,128]{1,0:T(8,128)(2,1)}, u32[]{:S(2)}) copy-start(bf16[640,128]{1,0:T(8,128)(2,1)} %router_ref.1) | copy-start | bytes 491524
  9.9 32.2 %copy-start.4 = (bf16[32,512]{1,0:T(8,128)(2,1)S(1)}, bf16[32,512]{1,0:T(8,128)(2,1)}, u32[]{:S(2)}) copy-start(bf16[32,512]{1,0:T(8,128)(2,1)} %key_ref.1) | copy-start | bytes 98308
  9.9 32.2 %copy-start.5 = (bf16[32,512]{1,0:T(8,128)(2,1)S(1)}, bf16[32,512]{1,0:T(8,128)(2,1)}, u32[]{:S(2)}) copy-start(bf16[32,512]{1,0:T(8,128)(2,1)} %value_ref.1) | copy-start | bytes 98308
  9.9 35.8 %copy-start.6 = (bf16[32,2560]{1,0:T(8,128)(2,1)S(1)}, bf16[32,2560]{1,0:T(8,128)(2,1)}, u32[]{:S(2)}) copy-start(bf16[32,2560]{1,0:T(8,128)(2,1)} %res_ref.3) | copy-start | bytes 491524
  10.0 9.9 %collective-permute-start.5 = (bf16[80,640]{1,0:T(8,128)(2,1)S(1)}, bf16[80,640]{1,0:T(8,128)(2,1)S(1)}, u32[]{:S(2)}, u32[]{:S(2)}) collective-permute-start(bf16[80,640]{1,0:T(8,128)(2,1)S(1)} %get-tuple-element.27), channel_id=1, source_target_pairs={{0,12},{1,15},{2,14},{3,13},{4,8},{5,11},{6,10},{7,9},{8,4},{9,7},... | collective-permute-start | bytes 307208 | tf_op jit(solution)/shard_map/ppermute | solution.py:368
  10.0 9.8 %collective-permute-start.6 = (bf16[80,640]{1,0:T(8,128)(2,1)S(1)}, bf16[80,640]{1,0:T(8,128)(2,1)S(1)}, u32[]{:S(2)}, u32[]{:S(2)}) collective-permute-start(bf16[80,640]{1,0:T(8,128)(2,1)S(1)} %collective-permute-done.2.refs_0_), channel_id=1, source_target_pairs={{0,1},{1,0},{2,3},{3,2},{4,5},{5,4},{6,7},{7,6},{8,9},{9,8},{10,11... | collective-permute-start | bytes 307208 | tf_op jit(solution)/shard_map/ppermute | solution.py:401
  13.3 6.6 %collective-permute-start.7 = (bf16[80,640]{1,0:T(8,128)(2,1)S(1)}, bf16[80,640]{1,0:T(8,128)(2,1)S(1)}, u32[]{:S(2)}, u32[]{:S(2)}) collective-permute-start(bf16[80,640]{1,0:T(8,128)(2,1)S(1)} %collective-permute-done.3.refs_1_), channel_id=1, source_target_pairs={{0,1},{1,0},{2,3},{3,2},{4,5},{5,4},{6,7},{7,6},{8,9},{9,8},{10,11... | collective-permute-start | bytes 307208 | tf_op jit(solution)/shard_map/ppermute | solution.py:401
  14.0 6.8 %collective-permute-start.8 = (bf16[80,640]{1,0:T(8,128)(2,1)S(1)}, bf16[80,640]{1,0:T(8,128)(2,1)S(1)}, u32[]{:S(2)}, u32[]{:S(2)}) collective-permute-start(bf16[80,640]{1,0:T(8,128)(2,1)S(1)} %collective-permute-done.4.refs_2_), channel_id=1, source_target_pairs={{0,1},{1,0},{2,3},{3,2},{4,5},{5,4},{6,7},{7,6},{8,9},{9,8},{10,11... | collective-permute-start | bytes 307208 | tf_op jit(solution)/shard_map/ppermute | solution.py:401
  19.9 1.3 %collective-permute-start.9 = (bf16[80,640]{1,0:T(8,128)(2,1)S(1)}, bf16[80,640]{1,0:T(8,128)(2,1)S(1)}, u32[]{:S(2)}, u32[]{:S(2)}) collective-permute-start(bf16[80,640]{1,0:T(8,128)(2,1)S(1)} %collective-permute-done.5.refs_3_), channel_id=1, source_target_pairs={{0,1},{1,0},{2,3},{3,2},{4,5},{5,4},{6,7},{7,6},{8,9},{9,8},{10,11... | collective-permute-start | bytes 307208 | tf_op jit(solution)/shard_map/ppermute | solution.py:401
  25.9 1.8 %collective-permute-start.10 = (bf16[320,640]{1,0:T(8,128)(2,1)S(1)}, bf16[320,640]{1,0:T(8,128)(2,1)S(1)}, u32[]{:S(2)}, u32[]{:S(2)}) collective-permute-start(bf16[320,640]{1,0:T(8,128)(2,1)S(1)} %get-tuple-element.29), channel_id=1, source_target_pairs={{0,1},{1,0},{2,3},{3,2},{4,5},{5,4},{6,7},{7,6},{8,9},{9,8},{10,11... | collective-permute-start | bytes 1228808 | tf_op jit(solution)/shard_map/ppermute | solution.py:421
  27.8 5.1 %collective-permute-start.11 = (bf16[80,640]{1,0:T(8,128)(2,1)S(1)}, bf16[80,640]{1,0:T(8,128)(2,1)S(1)}, u32[]{:S(2)}, u32[]{:S(2)}) collective-permute-start(bf16[80,640]{1,0:T(8,128)(2,1)S(1)} %get-tuple-element.30), channel_id=1, source_target_pairs={{0,0},{1,3},{2,2},{3,1},{4,4},{5,7},{6,6},{7,5},{8,8},{9,11},{10,1... | collective-permute-start | bytes 307208 | tf_op jit(solution)/shard_map/ppermute | solution.py:425
  28.5 7.1 %collective-permute-start.12 = (bf16[80,640]{1,0:T(8,128)(2,1)S(1)}, bf16[80,640]{1,0:T(8,128)(2,1)S(1)}, u32[]{:S(2)}, u32[]{:S(2)}) collective-permute-start(bf16[80,640]{1,0:T(8,128)(2,1)S(1)} %get-tuple-element.31), channel_id=1, source_target_pairs={{0,4},{1,7},{2,6},{3,5},{4,0},{5,3},{6,2},{7,1},{8,12},{9,15},{10,... | collective-permute-start | bytes 307208 | tf_op jit(solution)/shard_map/ppermute | solution.py:425
  30.2 7.0 %collective-permute-start.13 = (bf16[80,640]{1,0:T(8,128)(2,1)S(1)}, bf16[80,640]{1,0:T(8,128)(2,1)S(1)}, u32[]{:S(2)}, u32[]{:S(2)}) collective-permute-start(bf16[80,640]{1,0:T(8,128)(2,1)S(1)} %get-tuple-element.32), channel_id=1, source_target_pairs={{0,8},{1,11},{2,10},{3,9},{4,12},{5,15},{6,14},{7,13},{8,0},{9,3},... | collective-permute-start | bytes 307208 | tf_op jit(solution)/shard_map/ppermute | solution.py:425
  31.9 10.2 %collective-permute-start.14 = (bf16[80,640]{1,0:T(8,128)(2,1)S(1)}, bf16[80,640]{1,0:T(8,128)(2,1)S(1)}, u32[]{:S(2)}, u32[]{:S(2)}) collective-permute-start(bf16[80,640]{1,0:T(8,128)(2,1)S(1)} %get-tuple-element.33), channel_id=1, source_target_pairs={{0,12},{1,15},{2,14},{3,13},{4,8},{5,11},{6,10},{7,9},{8,4},{9,7},... | collective-permute-start | bytes 307208 | tf_op jit(solution)/shard_map/ppermute | solution.py:425
  32.9 12.8 %collective-permute-start.15 = (bf16[80,640]{1,0:T(8,128)(2,1)S(1)}, bf16[80,640]{1,0:T(8,128)(2,1)S(1)}, u32[]{:S(2)}, u32[]{:S(2)}) collective-permute-start(bf16[80,640]{1,0:T(8,128)(2,1)S(1)} %collective-permute-done.11.refs_0_), channel_id=1, source_target_pairs={{0,1},{1,0},{2,3},{3,2},{4,5},{5,4},{6,7},{7,6},{8,9},{9,8},{10,11... | collective-permute-start | bytes 307208 | tf_op jit(solution)/shard_map/ppermute | solution.py:426
  35.6 10.2 %collective-permute-start.16 = (bf16[80,640]{1,0:T(8,128)(2,1)S(1)}, bf16[80,640]{1,0:T(8,128)(2,1)S(1)}, u32[]{:S(2)}, u32[]{:S(2)}) collective-permute-start(bf16[80,640]{1,0:T(8,128)(2,1)S(1)} %collective-permute-done.12.refs_1_), channel_id=1, source_target_pairs={{0,1},{1,0},{2,3},{3,2},{4,5},{5,4},{6,7},{7,6},{8,9},{9,8},{10,11... | collective-permute-start | bytes 307208 | tf_op jit(solution)/shard_map/ppermute | solution.py:426
  37.2 8.5 %collective-permute-start.17 = (bf16[80,640]{1,0:T(8,128)(2,1)S(1)}, bf16[80,640]{1,0:T(8,128)(2,1)S(1)}, u32[]{:S(2)}, u32[]{:S(2)}) collective-permute-start(bf16[80,640]{1,0:T(8,128)(2,1)S(1)} %collective-permute-done.13.refs_2_), channel_id=1, source_target_pairs={{0,1},{1,0},{2,3},{3,2},{4,5},{5,4},{6,7},{7,6},{8,9},{9,8},{10,11... | collective-permute-start | bytes 307208 | tf_op jit(solution)/shard_map/ppermute | solution.py:426
  42.1 3.6 %collective-permute-start.18 = (bf16[80,640]{1,0:T(8,128)(2,1)S(1)}, bf16[80,640]{1,0:T(8,128)(2,1)S(1)}, u32[]{:S(2)}, u32[]{:S(2)}) collective-permute-start(bf16[80,640]{1,0:T(8,128)(2,1)S(1)} %collective-permute-done.14.refs_3_), channel_id=1, source_target_pairs={{0,1},{1,0},{2,3},{3,2},{4,5},{5,4},{6,7},{7,6},{8,9},{9,8},{10,11... | collective-permute-start | bytes 307208 | tf_op jit(solution)/shard_map/ppermute | solution.py:426

commit v2 on v1

--- a/solution.py
+++ b/solution.py
@@ -62,13 +62,39 @@
     return call
 
 
+def ring_place(pair, count):
+    return jnp.where((pair & 1) == 0, pair >> 1, count - 1 - (pair >> 1))
+
+
 def route_kernel(
-    ids_ref, res_ref, gain_ref, pos_ref, sel_ref, normed_ref, *, sub_local, per_owner, n_owner
+    ids_hbm_ref,
+    res_hbm_ref,
+    gain_hbm_ref,
+    pos_ref,
+    sel_ref,
+    normed_ref,
+    ids_ref,
+    res_ref,
+    gain_ref,
+    sem,
+    *,
+    sub_local,
+    per_owner,
+    n_owner,
 ):
+    fetches = [
+        pltpu.make_async_copy(source, target, sem.at[i])
+        for i, (source, target) in enumerate(
+            [(ids_hbm_ref, ids_ref), (res_hbm_ref, res_ref), (gain_hbm_ref, gain_ref)]
+        )
+    ]
+    for fetch in fetches:
+        fetch.start()
     owner = lax.axis_index("expert")
     mp = lax.axis_index("mp")
     tokens = ids_ref.shape[2]
     rows = tokens * SUB
+    fetches[0].wait()
     ids = jnp.concatenate([ids_ref[s].astype(F32) for s in range(SUB)], axis=0)
     ids = jnp.concatenate([ids, jnp.zeros((EXPERTS - SUB * TOP, tokens), F32)], axis=0)
     ids = jnp.concatenate([ids, jnp.zeros((EXPERTS, EXPERTS - tokens), F32)], axis=1).T
@@ -99,8 +125,9 @@
         total = total + jnp.sum(hot, axis=0, keepdims=True)
         slot = jnp.sum(hot * ahead, axis=1, keepdims=True).astype(jnp.int32)
         expert = jnp.sum(hot * lane_f, axis=1, keepdims=True).astype(jnp.int32)
-        apart = (expert >> log2(per_owner)) ^ owner
-        block = ((apart & 1) ^ mp) * half + (apart >> 1)
+        target = expert >> log2(per_owner)
+        step = (ring_place(target >> 1, half) - ring_place(owner >> 1, half)) & (half - 1)
+        block = ((target ^ owner ^ mp) & 1) * half + step
         flat = (block * CAP + slot) * per_owner + (expert & (per_owner - 1))
         packed = jnp.where(lane == k, flat.astype(F32), packed)
         packed = jnp.where(lane == TOP + k, expert.astype(F32), packed)
@@ -117,6 +144,8 @@
         hit = hit | (slot_row == turned[k : k + 1, :])
     sel_ref[...] = hit.astype(F32).astype(BF16)
     width = res_ref.shape[1] // sub_local
+    fetches[1].wait()
+    fetches[2].wait()
     for s, piece in enumerate(normed_rows(res_ref, gain_ref, sub_local, width)):
         normed_ref[s * tokens : (s + 1) * tokens, :] = piece
 
@@ -163,7 +192,7 @@
 
 
 def combine_kernel(pos_ref, weight_ref, res_ref, context_ref, *refs, sub_local, width):
-    blocks, out_ref = refs[:-1], refs[-1]
+    blocks, (out_hbm_ref, out_ref, sem) = refs[:-3], refs[-3:]
     tokens = res_ref.shape[0]
     rows = sub_local * tokens
     returned = jnp.concatenate([ref[...] for ref in blocks], axis=0)
@@ -175,10 +204,15 @@
         hot = (lane == flat).astype(F32).astype(BF16)
         picked = jnp.dot(hot, returned, preferred_element_type=F32)
         moe = moe + weight_ref[:, k : k + 1] * picked
+    stores = []
     for s in range(sub_local):
         at = slice(s * width, (s + 1) * width)
         total = res_ref[:, at].astype(F32) + context_ref[:, at]
         out_ref[:, at] = (total + moe[s * tokens : (s + 1) * tokens]).astype(BF16)
+        stores.append(pltpu.make_async_copy(out_ref.at[:, at], out_hbm_ref.at[:, at], sem.at[s]))
+        stores[-1].start()
+    for store in stores:
+        store.wait()
 
 
 def attend_kernel(
@@ -336,12 +370,17 @@
     gain = norm_gain.reshape(-1, HD)
 
     swap = [(0, 1), (1, 0)]
-    order = sorted(range(half), key=lambda j: (-j.bit_length(), j))
-
-    def partners(j):
-        return [
-            (e * n_mp + m, (e ^ (2 * j + m)) * n_mp + m) for e in range(n_owner) for m in range(n_mp)
-        ]
+    order = [half // 2] + [j for j in range(1, half) if j != half // 2] + [0]
+    ring = list(range(0, half, 2)) + list(range(1, half, 2))[::-1]
+
+    def partners(j, back=False):
+        pairs = []
+        for e in range(n_owner):
+            far = ring[(ring.index(e >> 1) + j) % half]
+            for m in range(n_mp):
+                pair = (e * n_mp + m, (2 * far + ((e ^ m) & 1)) * n_mp + m)
+                pairs.append(pair[::-1] if back else pair)
+        return pairs
 
     peer_residual = lax.ppermute(residual, "mp", swap)
     peer_gain = lax.ppermute(gain, "mp", swap)
@@ -352,7 +391,13 @@
             jax.ShapeDtypeStruct((half * slots, rows), BF16),
             jax.ShapeDtypeStruct((sub_local * tokens, width), BF16),
         ),
-        plain=(0, 1, 2),
+        hbm=(0, 1, 2),
+        scratch_shapes=(
+            pltpu.VMEM((SUB, TOP, tokens), jnp.int32),
+            pltpu.VMEM(residual.shape, BF16),
+            pltpu.VMEM(gain.shape, BF16),
+            pltpu.SemaphoreType.DMA((3,)),
+        ),
         cost=20.0,
         name="route",
     )(expert_ids.transpose(1, 2, 0), residual, gain)
@@ -398,35 +443,48 @@
         router_weight,
         pos,
     )
-    peer = [lax.ppermute(block, "mp", swap) for block in own]
-
-    mine, other = in_vmem(
-        functools.partial(ffn_kernel, n_block=n_owner, per_owner=per_owner),
-        (
-            jax.ShapeDtypeStruct((half * slots, width), F32),
-            jax.ShapeDtypeStruct((half * slots, width), BF16),
-        ),
-        scratch_shapes=(
-            pltpu.VMEM((width // HD, n_owner * slots, HD), F32),
-            pltpu.VMEM((width // HD, n_owner * slots, HD), F32),
-        ),
-        room=12 << 20,
-        cost=5.0,
-        name="ffn",
-    )(*own, *peer, expert_in, expert_out)
-    result = in_vmem(
-        reduce_kernel,
-        tuple(jax.ShapeDtypeStruct((slots, width), BF16) for _ in range(half)),
-        name="reduce",
-    )(mine, lax.ppermute(other, "mp", swap))
+    peer = [None] * half
+    for j in order:
+        peer[j] = lax.ppermute(own[j], "mp", swap)
+
+    def expert_pass(chosen, name):
+        mine, other = in_vmem(
+            functools.partial(ffn_kernel, n_block=2 * len(chosen), per_owner=per_owner),
+            (
+                jax.ShapeDtypeStruct((len(chosen) * slots, width), F32),
+                jax.ShapeDtypeStruct((len(chosen) * slots, width), BF16),
+            ),
+            scratch_shapes=(
+                pltpu.VMEM((width // HD, 2 * len(chosen) * slots, HD), F32),
+                pltpu.VMEM((width // HD, 2 * len(chosen) * slots, HD), F32),
+            ),
+            room=12 << 20,
+            cost=5.0,
+            name=name,
+        )(*[own[j] for j in chosen], *[peer[j] for j in chosen], expert_in, expert_out)
+        return in_vmem(
+            reduce_kernel,
+            tuple(jax.ShapeDtypeStruct((slots, width), BF16) for _ in chosen),
+            name="reduce",
+        )(mine, lax.ppermute(other, "mp", swap))
 
     back = [None] * half
+    early = order[: half // 2]
+    late = order[half // 2 :]
+    for chosen, name in ((early, "ffn_first"), (late, "ffn_last")):
+        for j, block in zip(chosen, expert_pass(chosen, name)):
+            back[j] = lax.ppermute(block, ("expert", "mp"), partners(j, back=True))
+    peer_back = [None] * half
     for j in order:
-        back[j] = lax.ppermute(result[j], ("expert", "mp"), partners(j))
-    peer_back = [lax.ppermute(block, "mp", swap) for block in back]
+        peer_back[j] = lax.ppermute(back[j], "mp", swap)
     (mixed,) = in_vmem(
         functools.partial(combine_kernel, sub_local=sub_local, width=width),
         (jax.ShapeDtypeStruct(residual.shape, BF16),),
+        hbm_out=(0,),
+        scratch_shapes=(
+            pltpu.VMEM(residual.shape, BF16),
+            pltpu.SemaphoreType.DMA((sub_local,)),
+        ),
         name="combine",
     )(pos, weights, residual, context, *back, *peer_back)
     return (attention, mixed)

time: 47.2 us -> 45.2 us (0.958)
  the two profiles are of different devices: /device:TPU:0 before, /device:TPU:17 now
where the time goes in v2:
time: 45.2 us; the launch traced here: 45 us
  starting transfers between devices  22.7 us (50%)
  Pallas kernels  15.4 us (34%)
  waiting for transfers between devices  5.7 us (13%)
  between operations  1.09 us (2%)
    pallas_call x8, Pallas kernels, call(): pl.pallas_call(kernel, out_shape=tuple((jax.ShapeDtypeStruct(s.shape, s.d...  15.4 us
    ppermute x4, starting transfers between devices, per_device(): own[j] = lax.ppermute(sent[j], ('expert', 'mp'), partners(j))  7.74 us
    ppermute x4, starting transfers between devices, per_device(): back[j] = lax.ppermute(block, ('expert', 'mp'), partners(j, back=True))  7.61 us
    ppermute x4, waiting for transfers between devices, per_device(): back[j] = lax.ppermute(block, ('expert', 'mp'), partners(j, back=True))  4.42 us
    ppermute x4, starting transfers between devices, per_device(): peer_back[j] = lax.ppermute(back[j], 'mp', swap)  2.98 us
    ppermute x4, starting transfers between devices, per_device(): peer[j] = lax.ppermute(own[j], 'mp', swap)  2.88 us
  transfers between devices with their start and end apart: 20, of which 4 were waited for; matrix products, arithmetic and copies ran while one was open for 0% of the time, Pallas kernels for 31%

profile of v2, /device:TPU:17, one launch (start us, length us, event | category | flops | bytes accessed | tf_op | source)
XLA Modules:
  0.0 45.0 jit_solution(12314305401784858143)
XLA Ops:
  0.6 0.7 %collective-permute-start.1 = (bf16[20,128]{1,0:T(8,128)(2,1)}, bf16[20,128]{1,0:T(8,128)(2,1)S(1)}, u32[]{:S(2)}, u32[]{:S(2)}) collective-permute-start(bf16[20,128]{1,0:T(8,128)(2,1)} %bitcast.7), channel_id=1, source_target_pairs={{0,1},{1,0},{2,3},{3,2},{4,5},{5,4},{6,7},{7,6},{8,9},{9,8},{10,11... | collective-permute-start | bytes 15368 | tf_op jit(solution)/shard_map/ppermute | solution.py:386
  1.4 0.1 collective-permute-start
  1.5 1.7 %route.1 = (f32[256,128]{1,0:T(8,128)S(1)}, bf16[320,256]{1,0:T(8,128)(2,1)S(1)}, bf16[128,640]{1,0:T(8,128)(2,1)S(1)}) custom-call(s32[8,2,32]{2,1,0:T(2,128)} %bitcast.6, bf16[32,2560]{1,0:T(8,128)(2,1)} %res_ref.1, bf16[20,128]{1,0:T(8,128)(2,1)} %bitcast.8), custom_call_target="tpu_custom_call" | custom-call | flops 10000000000 | bytes 60000000 | tf_op jit(solution)/shard_map/route/pallas_call | solution.py:44
  3.1 0.0 collective-permute-done.1.peer_gain_ref
  3.2 0.0 collective-permute-done.peer_ref
  3.2 0.0 slice-start.2
  3.2 0.0 slice-start.3
  3.2 0.0 slice-start.6
  3.2 0.0 slice-start.7
  3.2 0.4 dispatch.1
  3.6 1.2 %collective-permute-start.8 = (bf16[80,640]{1,0:T(8,128)(2,1)S(1)}, bf16[80,640]{1,0:T(8,128)(2,1)S(1)}, u32[]{:S(2)}, u32[]{:S(2)}) collective-permute-start(bf16[80,640]{1,0:T(8,128)(2,1)S(1)} %get-tuple-element.31), channel_id=1, source_target_pairs={{0,12},{1,15},{2,14},{3,13},{4,8},{5,11},{6,10},{7,9},{8,4},{9,7},... | collective-permute-start | bytes 307208 | tf_op jit(solution)/shard_map/ppermute | solution.py:413
  4.8 1.2 %collective-permute-start.9 = (bf16[80,640]{1,0:T(8,128)(2,1)S(1)}, bf16[80,640]{1,0:T(8,128)(2,1)S(1)}, u32[]{:S(2)}, u32[]{:S(2)}) collective-permute-start(bf16[80,640]{1,0:T(8,128)(2,1)S(1)} %get-tuple-element.32), channel_id=1, source_target_pairs={{0,8},{1,11},{2,10},{3,9},{4,0},{5,3},{6,2},{7,1},{8,12},{9,15},{1... | collective-permute-start | bytes 307208 | tf_op jit(solution)/shard_map/ppermute | solution.py:413
  6.0 2.1 %collective-permute-start.2 = (bf16[80,640]{1,0:T(8,128)(2,1)S(1)}, bf16[80,640]{1,0:T(8,128)(2,1)S(1)}, u32[]{:S(2)}, u32[]{:S(2)}) collective-permute-start(bf16[80,640]{1,0:T(8,128)(2,1)S(1)} %get-tuple-element.26), channel_id=1, source_target_pairs={{0,4},{1,7},{2,6},{3,5},{4,12},{5,15},{6,14},{7,13},{8,0},{9,3},{1... | collective-permute-start | bytes 307208 | tf_op jit(solution)/shard_map/ppermute | solution.py:413
  8.1 3.3 %collective-permute-start.3 = (bf16[80,640]{1,0:T(8,128)(2,1)S(1)}, bf16[80,640]{1,0:T(8,128)(2,1)S(1)}, u32[]{:S(2)}, u32[]{:S(2)}) collective-permute-start(bf16[80,640]{1,0:T(8,128)(2,1)S(1)} %get-tuple-element.27), channel_id=1, source_target_pairs={{0,0},{1,3},{2,2},{3,1},{4,4},{5,7},{6,6},{7,5},{8,8},{9,11},{10,1... | collective-permute-start | bytes 307208 | tf_op jit(solution)/shard_map/ppermute | solution.py:413
  11.4 0.5 %collective-permute-done.8.refs_0_ = bf16[80,640]{1,0:T(8,128)(2,1)S(1)} collective-permute-done((bf16[80,640]{1,0:T(8,128)(2,1)S(1)}, bf16[80,640]{1,0:T(8,128)(2,1)S(1)}, u32[]{:S(2)}, u32[]{:S(2)}) %collective-permute-start.8) | collective-permute-done | bytes 102432 | tf_op jit(solution)/shard_map/ppermute | solution.py:413
  11.9 2.3 %collective-permute-start.10 = (bf16[80,640]{1,0:T(8,128)(2,1)S(1)}, bf16[80,640]{1,0:T(8,128)(2,1)S(1)}, u32[]{:S(2)}, u32[]{:S(2)}) collective-permute-start(bf16[80,640]{1,0:T(8,128)(2,1)S(1)} %collective-permute-done.8.refs_0_), channel_id=1, source_target_pairs={{0,1},{1,0},{2,3},{3,2},{4,5},{5,4},{6,7},{7,6},{8,9},{9,8},{10,11... | collective-permute-start | bytes 307208 | tf_op jit(solution)/shard_map/ppermute | solution.py:448
  14.2 0.0 collective-permute-done.9.refs_1_
  14.2 0.0 collective-permute-start.11
  14.2 0.0 collective-permute-done.2.refs_0_
  14.2 0.5 %collective-permute-start.4 = (bf16[80,640]{1,0:T(8,128)(2,1)S(1)}, bf16[80,640]{1,0:T(8,128)(2,1)S(1)}, u32[]{:S(2)}, u32[]{:S(2)}) collective-permute-start(bf16[80,640]{1,0:T(8,128)(2,1)S(1)} %collective-permute-done.2.refs_0_), channel_id=1, source_target_pairs={{0,1},{1,0},{2,3},{3,2},{4,5},{5,4},{6,7},{7,6},{8,9},{9,8},{10,11... | collective-permute-start | bytes 307208 | tf_op jit(solution)/shard_map/ppermute | solution.py:448
  14.7 0.0 collective-permute-done.3.refs_1_
  14.7 0.1 collective-permute-start.5
  14.8 0.4 collective-permute-done.10.refs_2_
  15.1 0.4 collective-permute-done.11.refs_3_
  15.5 0.0 slice-done
  15.5 0.0 slice-done.1
  15.5 0.0 slice-done.4
  15.6 4.3 %ffn_first.1 = (f32[160,640]{1,0:T(8,128)S(1)}, bf16[160,640]{1,0:T(8,128)(2,1)S(1)}) custom-call(bf16[80,640]{1,0:T(8,128)(2,1)S(1)} %collective-permute-done.8.refs_0_, bf16[80,640]{1,0:T(8,128)(2,1)S(1)} %collective-permute-done.9.refs_1_, bf16[80,640]{1,0:T(8,128)(2,1)S(1)} %collective-permute-done.10.refs_2_, ...), custom_call_target="tpu_custom_call" | custom-call | flops 2500000000 | bytes 15000000 | tf_op jit(solution)/shard_map/ffn_first/pallas_call | solution.py:44
  19.8 0.0 copy-start
  19.9 0.0 copy-start.1
  19.9 0.0 copy-start.2
  19.9 0.0 copy-start.3
  19.9 0.0 copy-start.4
  19.9 0.0 copy-start.5
  19.9 0.0 copy-start.6
  19.9 0.2 collective-permute-start.12
  20.1 0.0 collective-permute-done.4.refs_2_
  20.1 0.0 collective-permute-done.5.refs_3_
  20.1 4.3 %ffn_last.1 = (f32[160,640]{1,0:T(8,128)S(1)}, bf16[160,640]{1,0:T(8,128)(2,1)S(1)}) custom-call(bf16[80,640]{1,0:T(8,128)(2,1)S(1)} %collective-permute-done.2.refs_0_, bf16[80,640]{1,0:T(8,128)(2,1)S(1)} %collective-permute-done.3.refs_1_, bf16[80,640]{1,0:T(8,128)(2,1)S(1)} %collective-permute-done.4.refs_2_, ...), custom_call_target="tpu_custom_call" | custom-call | flops 2500000000 | bytes 15000000 | tf_op jit(solution)/shard_map/ffn_last/pallas_call | solution.py:44
  24.4 0.4 collective-permute-start.6
  24.8 0.0 collective-permute-done.12.other_ref
  24.8 0.1 reduce.3
  24.9 2.8 %collective-permute-start.13 = (bf16[80,640]{1,0:T(8,128)(2,1)S(1)}, bf16[80,640]{1,0:T(8,128)(2,1)S(1)}, u32[]{:S(2)}, u32[]{:S(2)}) collective-permute-start(bf16[80,640]{1,0:T(8,128)(2,1)S(1)} %get-tuple-element.35), channel_id=1, source_target_pairs={{8,0},{11,1},{10,2},{9,3},{0,4},{3,5},{2,6},{1,7},{12,8},{15,9},{1... | collective-permute-start | bytes 307208 | tf_op jit(solution)/shard_map/ppermute | solution.py:476
  27.7 1.4 %collective-permute-start.14 = (bf16[80,640]{1,0:T(8,128)(2,1)S(1)}, bf16[80,640]{1,0:T(8,128)(2,1)S(1)}, u32[]{:S(2)}, u32[]{:S(2)}) collective-permute-start(bf16[80,640]{1,0:T(8,128)(2,1)S(1)} %get-tuple-element.36), channel_id=1, source_target_pairs={{12,0},{15,1},{14,2},{13,3},{8,4},{11,5},{10,6},{9,7},{4,8},{7,9},... | collective-permute-start | bytes 307208 | tf_op jit(solution)/shard_map/ppermute | solution.py:476
  29.1 0.0 collective-permute-done.6.other_ref
  29.1 0.1 reduce.2
  29.2 3.0 %collective-permute-start.7 = (bf16[80,640]{1,0:T(8,128)(2,1)S(1)}, bf16[80,640]{1,0:T(8,128)(2,1)S(1)}, u32[]{:S(2)}, u32[]{:S(2)}) collective-permute-start(bf16[80,640]{1,0:T(8,128)(2,1)S(1)} %get-tuple-element.30), channel_id=1, source_target_pairs={{0,0},{3,1},{2,2},{1,3},{4,4},{7,5},{6,6},{5,7},{8,8},{11,9},{10,1... | collective-permute-start | bytes 307208 | tf_op jit(solution)/shard_map/ppermute | solution.py:476
  32.2 0.4 collective-permute-start.15
  32.6 0.0 collective-permute-done.13.refs_1_
  32.6 1.6 %collective-permute-start.17 = (bf16[80,640]{1,0:T(8,128)(2,1)S(1)}, bf16[80,640]{1,0:T(8,128)(2,1)S(1)}, u32[]{:S(2)}, u32[]{:S(2)}) collective-permute-start(bf16[80,640]{1,0:T(8,128)(2,1)S(1)} %collective-permute-done.13.refs_1_), channel_id=1, source_target_pairs={{0,1},{1,0},{2,3},{3,2},{4,5},{5,4},{6,7},{7,6},{8,9},{9,8},{10,11... | collective-permute-start | bytes 307208 | tf_op jit(solution)/shard_map/ppermute | solution.py:479
  34.1 4.4 %collective-permute-done.14.refs_2_ = bf16[80,640]{1,0:T(8,128)(2,1)S(1)} collective-permute-done((bf16[80,640]{1,0:T(8,128)(2,1)S(1)}, bf16[80,640]{1,0:T(8,128)(2,1)S(1)}, u32[]{:S(2)}, u32[]{:S(2)}) %collective-permute-start.14) | collective-permute-done | bytes 102432 | tf_op jit(solution)/shard_map/ppermute | solution.py:476
  38.5 0.9 %collective-permute-start.18 = (bf16[80,640]{1,0:T(8,128)(2,1)S(1)}, bf16[80,640]{1,0:T(8,128)(2,1)S(1)}, u32[]{:S(2)}, u32[]{:S(2)}) collective-permute-start(bf16[80,640]{1,0:T(8,128)(2,1)S(1)} %collective-permute-done.14.refs_2_), channel_id=1, source_target_pairs={{0,1},{1,0},{2,3},{3,2},{4,5},{5,4},{6,7},{7,6},{8,9},{9,8},{10,11... | collective-permute-start | bytes 307208 | tf_op jit(solution)/shard_map/ppermute | solution.py:479
  39.5 0.0 collective-permute-done.7.refs_0_
  39.5 0.0 collective-permute-start.16
  39.5 0.0 collective-permute-done.15.refs_3_
  39.5 0.5 %collective-permute-start.19 = (bf16[80,640]{1,0:T(8,128)(2,1)S(1)}, bf16[80,640]{1,0:T(8,128)(2,1)S(1)}, u32[]{:S(2)}, u32[]{:S(2)}) collective-permute-start(bf16[80,640]{1,0:T(8,128)(2,1)S(1)} %collective-permute-done.15.refs_3_), channel_id=1, source_target_pairs={{0,1},{1,0},{2,3},{3,2},{4,5},{5,4},{6,7},{7,6},{8,9},{9,8},{10,11... | collective-permute-start | bytes 307208 | tf_op jit(solution)/shard_map/ppermute | solution.py:479
  40.0 0.0 copy-done
  40.0 0.0 copy-done.2
  40.0 3.5 %attend.1 = (bf16[32,2560]{1,0:T(8,128)(2,1)}, f32[32,2560]{1,0:T(8,128)S(1)}, f32[128,128]{1,0:T(8,128)S(1)}) custom-call(s32[32]{0:T(128)} %length_ref.1, bf16[32,2560]{1,0:T(8,128)(2,1)S(1)} %copy-done.2, bf16[32,512]{1,0:T(8,128)(2,1)S(1)} %copy-done.4, bf16[32,512]{1,0:T(8,128)(2,1)S(1)} %copy-done.5, bf16[32,128,512]{2,1,0:T(8,128)(2,1)S(1)} %copy-done, ...), custom_call_target="tpu_custom_call" | custom-call | flops 2000000000 | bytes 12000000 | tf_op jit(solution)/shard_map/attend/pallas_call | solution.py:44
  43.6 0.0 collective-permute-done.17.refs_5_
  43.6 0.0 collective-permute-done.18.refs_6_
  43.6 0.0 collective-permute-done.16.refs_4_
  43.6 0.0 collective-permute-done.19.refs_7_
  43.6 1.2 %combine.1 = bf16[32,2560]{1,0:T(8,128)(2,1)} custom-call(f32[256,128]{1,0:T(8,128)S(1)} %get-tuple-element.21.pos_ref, f32[128,128]{1,0:T(8,128)S(1)} %get-tuple-element.23.weight_ref, bf16[32,2560]{1,0:T(8,128)(2,1)S(1)} %copy-done.6, f32[32,2560]{1,0:T(8,128)S(1)} %get-tuple-element.24.context_ref, bf16[80,640]{1,0:T(8,128)(2,1)S(1)} %collective-permute-done.7.refs_0_, ...), custom_call_target="tpu_custom_call" | custom-call | flops 500000000 | bytes 3000000 | tf_op jit(solution)/shard_map/combine/pallas_call | solution.py:44
  (16 shorter events, 0.0 us)
Async XLA Ops:
  0.6 2.5 %collective-permute-start.1 = (bf16[20,128]{1,0:T(8,128)(2,1)}, bf16[20,128]{1,0:T(8,128)(2,1)S(1)}, u32[]{:S(2)}, u32[]{:S(2)}) collective-permute-start(bf16[20,128]{1,0:T(8,128)(2,1)} %bitcast.7), channel_id=1, source_target_pairs={{0,1},{1,0},{2,3},{3,2},{4,5},{5,4},{6,7},{7,6},{8,9},{9,8},{10,11... | collective-permute-start | bytes 15368 | tf_op jit(solution)/shard_map/ppermute | solution.py:386
  1.4 1.8 %collective-permute-start = (bf16[32,2560]{1,0:T(8,128)(2,1)}, bf16[32,2560]{1,0:T(8,128)(2,1)S(1)}, u32[]{:S(2)}, u32[]{:S(2)}) collective-permute-start(bf16[32,2560]{1,0:T(8,128)(2,1)} %res_ref.1), channel_id=1, source_target_pairs={{0,1},{1,0},{2,3},{3,2},{4,5},{5,4},{6,7},{7,6},{8,9},{9,8},{10,11... | collective-permute-start | bytes 491528 | tf_op jit(solution)/shard_map/ppermute | solution.py:385
  1.4 14.1 %slice-start = ((s8[13107200]{0:T(1024)(128)(4,1)}), s8[4194304]{0:T(1024)(128)(4,1)S(1)}, s32[]{:S(2)}) async-start(s8[13107200]{0:T(1024)(128)(4,1)} %bitcast.2), calls=%async_computation | async-start | bytes 8388608
  1.5 14.1 %slice-start.1 = ((s8[13107200]{0:T(1024)(128)(4,1)}), s8[4194304]{0:T(1024)(128)(4,1)S(1)}, s32[]{:S(2)}) async-start(s8[13107200]{0:T(1024)(128)(4,1)} %bitcast.2), calls=%async_computation.1 | async-start | bytes 8388608
  1.5 14.1 %slice-start.4 = ((s8[13107200]{0:T(1024)(128)(4,1)}), s8[4194304]{0:T(1024)(128)(4,1)S(1)}, s32[]{:S(2)}) async-start(s8[13107200]{0:T(1024)(128)(4,1)} %bitcast.4), calls=%async_computation.4 | async-start | bytes 8388608
  1.5 14.1 %slice-start.5 = ((s8[13107200]{0:T(1024)(128)(4,1)}), s8[4194304]{0:T(1024)(128)(4,1)S(1)}, s32[]{:S(2)}) async-start(s8[13107200]{0:T(1024)(128)(4,1)} %bitcast.4), calls=%async_computation.5 | async-start | bytes 8388608
  3.2 12.4 %slice-start.2 = ((s8[13107200]{0:T(1024)(128)(4,1)}), s8[4194304]{0:T(1024)(128)(4,1)S(1)}, s32[]{:S(2)}) async-start(s8[13107200]{0:T(1024)(128)(4,1)} %bitcast.2), calls=%async_computation.2 | async-start | bytes 8388608
  3.2 12.3 %slice-start.3 = ((s8[13107200]{0:T(1024)(128)(4,1)}), s8[524288]{0:T(1024)(128)(4,1)S(1)}, s32[]{:S(2)}) async-start(s8[13107200]{0:T(1024)(128)(4,1)} %bitcast.2), calls=%async_computation.3 | async-start | bytes 1048576
  3.2 12.3 %slice-start.6 = ((s8[13107200]{0:T(1024)(128)(4,1)}), s8[4194304]{0:T(1024)(128)(4,1)S(1)}, s32[]{:S(2)}) async-start(s8[13107200]{0:T(1024)(128)(4,1)} %bitcast.4), calls=%async_computation.6 | async-start | bytes 8388608
  3.2 12.3 %slice-start.7 = ((s8[13107200]{0:T(1024)(128)(4,1)}), s8[524288]{0:T(1024)(128)(4,1)S(1)}, s32[]{:S(2)}) async-start(s8[13107200]{0:T(1024)(128)(4,1)} %bitcast.4), calls=%async_computation.7 | async-start | bytes 1048576
  3.6 8.3 %collective-permute-start.8 = (bf16[80,640]{1,0:T(8,128)(2,1)S(1)}, bf16[80,640]{1,0:T(8,128)(2,1)S(1)}, u32[]{:S(2)}, u32[]{:S(2)}) collective-permute-start(bf16[80,640]{1,0:T(8,128)(2,1)S(1)} %get-tuple-element.31), channel_id=1, source_target_pairs={{0,12},{1,15},{2,14},{3,13},{4,8},{5,11},{6,10},{7,9},{8,4},{9,7},... | collective-permute-start | bytes 307208 | tf_op jit(solution)/shard_map/ppermute | solution.py:413
  4.8 9.4 %collective-permute-start.9 = (bf16[80,640]{1,0:T(8,128)(2,1)S(1)}, bf16[80,640]{1,0:T(8,128)(2,1)S(1)}, u32[]{:S(2)}, u32[]{:S(2)}) collective-permute-start(bf16[80,640]{1,0:T(8,128)(2,1)S(1)} %get-tuple-element.32), channel_id=1, source_target_pairs={{0,8},{1,11},{2,10},{3,9},{4,0},{5,3},{6,2},{7,1},{8,12},{9,15},{1... | collective-permute-start | bytes 307208 | tf_op jit(solution)/shard_map/ppermute | solution.py:413
  6.0 8.2 %collective-permute-start.2 = (bf16[80,640]{1,0:T(8,128)(2,1)S(1)}, bf16[80,640]{1,0:T(8,128)(2,1)S(1)}, u32[]{:S(2)}, u32[]{:S(2)}) collective-permute-start(bf16[80,640]{1,0:T(8,128)(2,1)S(1)} %get-tuple-element.26), channel_id=1, source_target_pairs={{0,4},{1,7},{2,6},{3,5},{4,12},{5,15},{6,14},{7,13},{8,0},{9,3},{1... | collective-permute-start | bytes 307208 | tf_op jit(solution)/shard_map/ppermute | solution.py:413
  8.1 6.7 %collective-permute-start.3 = (bf16[80,640]{1,0:T(8,128)(2,1)S(1)}, bf16[80,640]{1,0:T(8,128)(2,1)S(1)}, u32[]{:S(2)}, u32[]{:S(2)}) collective-permute-start(bf16[80,640]{1,0:T(8,128)(2,1)S(1)} %get-tuple-element.27), channel_id=1, source_target_pairs={{0,0},{1,3},{2,2},{3,1},{4,4},{5,7},{6,6},{7,5},{8,8},{9,11},{10,1... | collective-permute-start | bytes 307208 | tf_op jit(solution)/shard_map/ppermute | solution.py:413
  11.9 3.3 %collective-permute-start.10 = (bf16[80,640]{1,0:T(8,128)(2,1)S(1)}, bf16[80,640]{1,0:T(8,128)(2,1)S(1)}, u32[]{:S(2)}, u32[]{:S(2)}) collective-permute-start(bf16[80,640]{1,0:T(8,128)(2,1)S(1)} %collective-permute-done.8.refs_0_), channel_id=1, source_target_pairs={{0,1},{1,0},{2,3},{3,2},{4,5},{5,4},{6,7},{7,6},{8,9},{9,8},{10,11... | collective-permute-start | bytes 307208 | tf_op jit(solution)/shard_map/ppermute | solution.py:448
  14.2 1.3 %collective-permute-start.11 = (bf16[80,640]{1,0:T(8,128)(2,1)S(1)}, bf16[80,640]{1,0:T(8,128)(2,1)S(1)}, u32[]{:S(2)}, u32[]{:S(2)}) collective-permute-start(bf16[80,640]{1,0:T(8,128)(2,1)S(1)} %collective-permute-done.9.refs_1_), channel_id=1, source_target_pairs={{0,1},{1,0},{2,3},{3,2},{4,5},{5,4},{6,7},{7,6},{8,9},{9,8},{10,11... | collective-permute-start | bytes 307208 | tf_op jit(solution)/shard_map/ppermute | solution.py:448
  14.2 5.9 %collective-permute-start.4 = (bf16[80,640]{1,0:T(8,128)(2,1)S(1)}, bf16[80,640]{1,0:T(8,128)(2,1)S(1)}, u32[]{:S(2)}, u32[]{:S(2)}) collective-permute-start(bf16[80,640]{1,0:T(8,128)(2,1)S(1)} %collective-permute-done.2.refs_0_), channel_id=1, source_target_pairs={{0,1},{1,0},{2,3},{3,2},{4,5},{5,4},{6,7},{7,6},{8,9},{9,8},{10,11... | collective-permute-start | bytes 307208 | tf_op jit(solution)/shard_map/ppermute | solution.py:448
  14.7 5.4 %collective-permute-start.5 = (bf16[80,640]{1,0:T(8,128)(2,1)S(1)}, bf16[80,640]{1,0:T(8,128)(2,1)S(1)}, u32[]{:S(2)}, u32[]{:S(2)}) collective-permute-start(bf16[80,640]{1,0:T(8,128)(2,1)S(1)} %collective-permute-done.3.refs_1_), channel_id=1, source_target_pairs={{0,1},{1,0},{2,3},{3,2},{4,5},{5,4},{6,7},{7,6},{8,9},{9,8},{10,11... | collective-permute-start | bytes 307208 | tf_op jit(solution)/shard_map/ppermute | solution.py:448
  19.8 20.1 %copy-start = (bf16[32,128,512]{2,1,0:T(8,128)(2,1)S(1)}, bf16[32,128,512]{2,1,0:T(8,128)(2,1)}, u32[]{:S(2)}) copy-start(bf16[32,128,512]{2,1,0:T(8,128)(2,1)} %cache_key_ref.1) | copy-start | bytes 12582916
  19.9 20.1 %copy-start.1 = (bf16[32,128,512]{2,1,0:T(8,128)(2,1)S(1)}, bf16[32,128,512]{2,1,0:T(8,128)(2,1)}, u32[]{:S(2)}) copy-start(bf16[32,128,512]{2,1,0:T(8,128)(2,1)} %cache_value_ref.1) | copy-start | bytes 12582916
  19.9 20.1 %copy-start.2 = (bf16[32,2560]{1,0:T(8,128)(2,1)S(1)}, bf16[32,2560]{1,0:T(8,128)(2,1)}, u32[]{:S(2)}) copy-start(bf16[32,2560]{1,0:T(8,128)(2,1)} %query_ref.1) | copy-start | bytes 491524
  19.9 20.1 %copy-start.3 = (bf16[640,128]{1,0:T(8,128)(2,1)S(1)}, bf16[640,128]{1,0:T(8,128)(2,1)}, u32[]{:S(2)}) copy-start(bf16[640,128]{1,0:T(8,128)(2,1)} %router_ref.1) | copy-start | bytes 491524
  19.9 20.1 %copy-start.4 = (bf16[32,512]{1,0:T(8,128)(2,1)S(1)}, bf16[32,512]{1,0:T(8,128)(2,1)}, u32[]{:S(2)}) copy-start(bf16[32,512]{1,0:T(8,128)(2,1)} %key_ref.1) | copy-start | bytes 98308
  19.9 20.1 %copy-start.5 = (bf16[32,512]{1,0:T(8,128)(2,1)S(1)}, bf16[32,512]{1,0:T(8,128)(2,1)}, u32[]{:S(2)}) copy-start(bf16[32,512]{1,0:T(8,128)(2,1)} %value_ref.1) | copy-start | bytes 98308
  19.9 23.7 %copy-start.6 = (bf16[32,2560]{1,0:T(8,128)(2,1)S(1)}, bf16[32,2560]{1,0:T(8,128)(2,1)}, u32[]{:S(2)}) copy-start(bf16[32,2560]{1,0:T(8,128)(2,1)} %res_ref.1) | copy-start | bytes 491524
  19.9 4.9 %collective-permute-start.12 = (bf16[160,640]{1,0:T(8,128)(2,1)S(1)}, bf16[160,640]{1,0:T(8,128)(2,1)S(1)}, u32[]{:S(2)}, u32[]{:S(2)}) collective-permute-start(bf16[160,640]{1,0:T(8,128)(2,1)S(1)} %get-tuple-element.34), channel_id=1, source_target_pairs={{0,1},{1,0},{2,3},{3,2},{4,5},{5,4},{6,7},{7,6},{8,9},{9,8},{10,11... | collective-permute-start | bytes 614408 | tf_op jit(solution)/shard_map/ppermute | solution.py:469
  24.4 4.7 %collective-permute-start.6 = (bf16[160,640]{1,0:T(8,128)(2,1)S(1)}, bf16[160,640]{1,0:T(8,128)(2,1)S(1)}, u32[]{:S(2)}, u32[]{:S(2)}) collective-permute-start(bf16[160,640]{1,0:T(8,128)(2,1)S(1)} %get-tuple-element.29), channel_id=1, source_target_pairs={{0,1},{1,0},{2,3},{3,2},{4,5},{5,4},{6,7},{7,6},{8,9},{9,8},{10,11... | collective-permute-start | bytes 614408 | tf_op jit(solution)/shard_map/ppermute | solution.py:469
  24.9 7.7 %collective-permute-start.13 = (bf16[80,640]{1,0:T(8,128)(2,1)S(1)}, bf16[80,640]{1,0:T(8,128)(2,1)S(1)}, u32[]{:S(2)}, u32[]{:S(2)}) collective-permute-start(bf16[80,640]{1,0:T(8,128)(2,1)S(1)} %get-tuple-element.35), channel_id=1, source_target_pairs={{8,0},{11,1},{10,2},{9,3},{0,4},{3,5},{2,6},{1,7},{12,8},{15,9},{1... | collective-permute-start | bytes 307208 | tf_op jit(solution)/shard_map/ppermute | solution.py:476
  27.7 10.8 %collective-permute-start.14 = (bf16[80,640]{1,0:T(8,128)(2,1)S(1)}, bf16[80,640]{1,0:T(8,128)(2,1)S(1)}, u32[]{:S(2)}, u32[]{:S(2)}) collective-permute-start(bf16[80,640]{1,0:T(8,128)(2,1)S(1)} %get-tuple-element.36), channel_id=1, source_target_pairs={{12,0},{15,1},{14,2},{13,3},{8,4},{11,5},{10,6},{9,7},{4,8},{7,9},... | collective-permute-start | bytes 307208 | tf_op jit(solution)/shard_map/ppermute | solution.py:476
  29.2 10.3 %collective-permute-start.7 = (bf16[80,640]{1,0:T(8,128)(2,1)S(1)}, bf16[80,640]{1,0:T(8,128)(2,1)S(1)}, u32[]{:S(2)}, u32[]{:S(2)}) collective-permute-start(bf16[80,640]{1,0:T(8,128)(2,1)S(1)} %get-tuple-element.30), channel_id=1, source_target_pairs={{0,0},{3,1},{2,2},{1,3},{4,4},{7,5},{6,6},{5,7},{8,8},{11,9},{10,1... | collective-permute-start | bytes 307208 | tf_op jit(solution)/shard_map/ppermute | solution.py:476
  32.2 7.3 %collective-permute-start.15 = (bf16[80,640]{1,0:T(8,128)(2,1)S(1)}, bf16[80,640]{1,0:T(8,128)(2,1)S(1)}, u32[]{:S(2)}, u32[]{:S(2)}) collective-permute-start(bf16[80,640]{1,0:T(8,128)(2,1)S(1)} %get-tuple-element.37), channel_id=1, source_target_pairs={{4,0},{7,1},{6,2},{5,3},{12,4},{15,5},{14,6},{13,7},{0,8},{3,9},{2... | collective-permute-start | bytes 307208 | tf_op jit(solution)/shard_map/ppermute | solution.py:476
  32.6 11.0 %collective-permute-start.17 = (bf16[80,640]{1,0:T(8,128)(2,1)S(1)}, bf16[80,640]{1,0:T(8,128)(2,1)S(1)}, u32[]{:S(2)}, u32[]{:S(2)}) collective-permute-start(bf16[80,640]{1,0:T(8,128)(2,1)S(1)} %collective-permute-done.13.refs_1_), channel_id=1, source_target_pairs={{0,1},{1,0},{2,3},{3,2},{4,5},{5,4},{6,7},{7,6},{8,9},{9,8},{10,11... | collective-permute-start | bytes 307208 | tf_op jit(solution)/shard_map/ppermute | solution.py:479
  38.5 5.0 %collective-permute-start.18 = (bf16[80,640]{1,0:T(8,128)(2,1)S(1)}, bf16[80,640]{1,0:T(8,128)(2,1)S(1)}, u32[]{:S(2)}, u32[]{:S(2)}) collective-permute-start(bf16[80,640]{1,0:T(8,128)(2,1)S(1)} %collective-permute-done.14.refs_2_), channel_id=1, source_target_pairs={{0,1},{1,0},{2,3},{3,2},{4,5},{5,4},{6,7},{7,6},{8,9},{9,8},{10,11... | collective-permute-start | bytes 307208 | tf_op jit(solution)/shard_map/ppermute | solution.py:479
  39.5 4.1 %collective-permute-start.16 = (bf16[80,640]{1,0:T(8,128)(2,1)S(1)}, bf16[80,640]{1,0:T(8,128)(2,1)S(1)}, u32[]{:S(2)}, u32[]{:S(2)}) collective-permute-start(bf16[80,640]{1,0:T(8,128)(2,1)S(1)} %collective-permute-done.7.refs_0_), channel_id=1, source_target_pairs={{0,1},{1,0},{2,3},{3,2},{4,5},{5,4},{6,7},{7,6},{8,9},{9,8},{10,11... | collective-permute-start | bytes 307208 | tf_op jit(solution)/shard_map/ppermute | solution.py:479
  39.5 4.1 %collective-permute-start.19 = (bf16[80,640]{1,0:T(8,128)(2,1)S(1)}, bf16[80,640]{1,0:T(8,128)(2,1)S(1)}, u32[]{:S(2)}, u32[]{:S(2)}) collective-permute-start(bf16[80,640]{1,0:T(8,128)(2,1)S(1)} %collective-permute-done.15.refs_3_), channel_id=1, source_target_pairs={{0,1},{1,0},{2,3},{3,2},{4,5},{5,4},{6,7},{7,6},{8,9},{9,8},{10,11... | collective-permute-start | bytes 307208 | tf_op jit(solution)/shard_map/ppermute | solution.py:479

commit v3 on v2

--- a/solution.py
+++ b/solution.py
@@ -236,7 +236,7 @@
     store_sem,
 ):
     tokens = query_ref.shape[0]
-    unroll = math.gcd(tokens, 16)
+    unroll = math.gcd(tokens, 32)
     groups = key_ref.shape[1] // HD
     per_group = HEADS // KV_HEADS
     heads = groups * per_group
@@ -469,11 +469,8 @@
         )(mine, lax.ppermute(other, "mp", swap))
 
     back = [None] * half
-    early = order[: half // 2]
-    late = order[half // 2 :]
-    for chosen, name in ((early, "ffn_first"), (late, "ffn_last")):
-        for j, block in zip(chosen, expert_pass(chosen, name)):
-            back[j] = lax.ppermute(block, ("expert", "mp"), partners(j, back=True))
+    for j, block in zip(order, expert_pass(order, "ffn")):
+        back[j] = lax.ppermute(block, ("expert", "mp"), partners(j, back=True))
     peer_back = [None] * half
     for j in order:
         peer_back[j] = lax.ppermute(back[j], "mp", swap)

time: 45.2 us -> 45.4 us (level)
  the two profiles are of different devices: /device:TPU:17 before, /device:TPU:0 now
where the time goes in v3:
time: 45.4 us; the launch traced here: 45.2 us
  starting transfers between devices  25.9 us (57%)
  Pallas kernels  11.4 us (25%)
  waiting for transfers between devices  6.95 us (15%)
  between operations  0.89 us (2%)
    pallas_call x6, Pallas kernels, call(): pl.pallas_call(kernel, out_shape=tuple((jax.ShapeDtypeStruct(s.shape, s.d...  11.4 us
    ppermute x4, starting transfers between devices, per_device(): peer_back[j] = lax.ppermute(back[j], 'mp', swap)  8.96 us
    ppermute x4, starting transfers between devices, per_device(): own[j] = lax.ppermute(sent[j], ('expert', 'mp'), partners(j))  7.9 us
    ppermute x4, starting transfers between devices, per_device(): back[j] = lax.ppermute(block, ('expert', 'mp'), partners(j, back=True))  5.22 us
    ppermute x4, waiting for transfers between devices, per_device(): own[j] = lax.ppermute(sent[j], ('expert', 'mp'), partners(j))  4.6 us
    ppermute x4, starting transfers between devices, per_device(): peer[j] = lax.ppermute(own[j], 'mp', swap)  2.73 us
    ppermute x1, waiting for transfers between devices, expert_pass(): lax.ppermute(other, 'mp', swap)  1.38 us
    ppermute x4, waiting for transfers between devices, per_device(): peer[j] = lax.ppermute(own[j], 'mp', swap)  0.95 us
  transfers between devices with their start and end apart: 19, of which 6 were waited for; matrix products, arithmetic and copies ran while one was open for 0% of the time, Pallas kernels for 11%

profile of v3, /device:TPU:0, one launch (start us, length us, event | category | flops | bytes accessed | tf_op | source)
XLA Modules:
  0.0 45.2 jit_solution(12745850821108940973)
XLA Ops:
  0.6 0.6 %collective-permute-start.1 = (bf16[20,128]{1,0:T(8,128)(2,1)}, bf16[20,128]{1,0:T(8,128)(2,1)S(1)}, u32[]{:S(2)}, u32[]{:S(2)}) collective-permute-start(bf16[20,128]{1,0:T(8,128)(2,1)} %bitcast.7), channel_id=1, source_target_pairs={{0,1},{1,0},{2,3},{3,2},{4,5},{5,4},{6,7},{7,6},{8,9},{9,8},{10,11... | collective-permute-start | bytes 15368 | tf_op jit(solution)/shard_map/ppermute | solution.py:386
  1.2 0.1 collective-permute-start
  1.3 1.7 %route.1 = (f32[256,128]{1,0:T(8,128)S(1)}, bf16[320,256]{1,0:T(8,128)(2,1)S(1)}, bf16[128,640]{1,0:T(8,128)(2,1)S(1)}) custom-call(s32[8,2,32]{2,1,0:T(2,128)} %bitcast.6, bf16[32,2560]{1,0:T(8,128)(2,1)} %res_ref.1, bf16[20,128]{1,0:T(8,128)(2,1)} %bitcast.8), custom_call_target="tpu_custom_call" | custom-call | flops 10000000000 | bytes 60000000 | tf_op jit(solution)/shard_map/route/pallas_call | solution.py:44
  3.0 0.0 collective-permute-done.1.peer_gain_ref
  3.0 0.0 collective-permute-done.peer_ref
  3.0 0.0 slice-start.2
  3.0 0.0 slice-start.3
  3.0 0.0 slice-start.6
  3.0 0.0 slice-start.7
  3.0 0.4 dispatch.1
  3.4 5.1 %collective-permute-start.2 = (bf16[80,640]{1,0:T(8,128)(2,1)S(1)}, bf16[80,640]{1,0:T(8,128)(2,1)S(1)}, u32[]{:S(2)}, u32[]{:S(2)}) collective-permute-start(bf16[80,640]{1,0:T(8,128)(2,1)S(1)} %get-tuple-element.24), channel_id=1, source_target_pairs={{0,12},{1,15},{2,14},{3,13},{4,8},{5,11},{6,10},{7,9},{8,4},{9,7},... | collective-permute-start | bytes 307208 | tf_op jit(solution)/shard_map/ppermute | solution.py:413
  8.5 0.0 collective-permute-start.3
  8.5 2.0 %collective-permute-start.4 = (bf16[80,640]{1,0:T(8,128)(2,1)S(1)}, bf16[80,640]{1,0:T(8,128)(2,1)S(1)}, u32[]{:S(2)}, u32[]{:S(2)}) collective-permute-start(bf16[80,640]{1,0:T(8,128)(2,1)S(1)} %get-tuple-element.26), channel_id=1, source_target_pairs={{0,4},{1,7},{2,6},{3,5},{4,12},{5,15},{6,14},{7,13},{8,0},{9,3},{1... | collective-permute-start | bytes 307208 | tf_op jit(solution)/shard_map/ppermute | solution.py:413
  10.5 0.0 copy-start.4
  10.6 0.0 copy-start.5
  10.6 0.0 copy-start.6
  10.6 0.8 %collective-permute-start.5 = (bf16[80,640]{1,0:T(8,128)(2,1)S(1)}, bf16[80,640]{1,0:T(8,128)(2,1)S(1)}, u32[]{:S(2)}, u32[]{:S(2)}) collective-permute-start(bf16[80,640]{1,0:T(8,128)(2,1)S(1)} %get-tuple-element.27), channel_id=1, source_target_pairs={{0,0},{1,3},{2,2},{3,1},{4,4},{5,7},{6,6},{7,5},{8,8},{9,11},{10,1... | collective-permute-start | bytes 307208 | tf_op jit(solution)/shard_map/ppermute | solution.py:413
  11.4 0.7 %collective-permute-done.2.refs_0_ = bf16[80,640]{1,0:T(8,128)(2,1)S(1)} collective-permute-done((bf16[80,640]{1,0:T(8,128)(2,1)S(1)}, bf16[80,640]{1,0:T(8,128)(2,1)S(1)}, u32[]{:S(2)}, u32[]{:S(2)}) %collective-permute-start.2) | collective-permute-done | bytes 102432 | tf_op jit(solution)/shard_map/ppermute | solution.py:413
  12.1 2.2 %collective-permute-start.6 = (bf16[80,640]{1,0:T(8,128)(2,1)S(1)}, bf16[80,640]{1,0:T(8,128)(2,1)S(1)}, u32[]{:S(2)}, u32[]{:S(2)}) collective-permute-start(bf16[80,640]{1,0:T(8,128)(2,1)S(1)} %collective-permute-done.2.refs_0_), channel_id=1, source_target_pairs={{0,1},{1,0},{2,3},{3,2},{4,5},{5,4},{6,7},{7,6},{8,9},{9,8},{10,11... | collective-permute-start | bytes 307208 | tf_op jit(solution)/shard_map/ppermute | solution.py:448
  14.3 0.2 collective-permute-done.3.refs_1_
  14.5 0.0 collective-permute-start.7
  14.5 3.7 %collective-permute-done.4.refs_2_ = bf16[80,640]{1,0:T(8,128)(2,1)S(1)} collective-permute-done((bf16[80,640]{1,0:T(8,128)(2,1)S(1)}, bf16[80,640]{1,0:T(8,128)(2,1)S(1)}, u32[]{:S(2)}, u32[]{:S(2)}) %collective-permute-start.4) | collective-permute-done | bytes 102432 | tf_op jit(solution)/shard_map/ppermute | solution.py:413
  18.2 0.0 collective-permute-start.8
  18.2 0.0 collective-permute-done.5.refs_3_
  18.2 0.5 %collective-permute-start.9 = (bf16[80,640]{1,0:T(8,128)(2,1)S(1)}, bf16[80,640]{1,0:T(8,128)(2,1)S(1)}, u32[]{:S(2)}, u32[]{:S(2)}) collective-permute-start(bf16[80,640]{1,0:T(8,128)(2,1)S(1)} %collective-permute-done.5.refs_3_), channel_id=1, source_target_pairs={{0,1},{1,0},{2,3},{3,2},{4,5},{5,4},{6,7},{7,6},{8,9},{9,8},{10,11... | collective-permute-start | bytes 307208 | tf_op jit(solution)/shard_map/ppermute | solution.py:448
  18.7 0.0 collective-permute-done.6.refs_4_
  18.7 0.0 collective-permute-done.7.refs_5_
  18.7 0.8 %collective-permute-done.8.refs_6_ = bf16[80,640]{1,0:T(8,128)(2,1)S(1)} collective-permute-done((bf16[80,640]{1,0:T(8,128)(2,1)S(1)}, bf16[80,640]{1,0:T(8,128)(2,1)S(1)}, u32[]{:S(2)}, u32[]{:S(2)}) %collective-permute-start.8) | collective-permute-done | bytes 102432 | tf_op jit(solution)/shard_map/ppermute | solution.py:448
  19.5 0.2 collective-permute-done.9.refs_7_
  19.7 0.0 slice-done
  19.7 0.0 slice-done.1
  19.7 0.0 slice-done.4
  19.7 0.0 slice-done.5
  19.7 0.0 slice-done.2
  19.7 0.0 slice-done.3
  19.7 0.0 slice-done.6
  19.7 0.0 slice-done.7
  19.7 4.6 %ffn.1 = (f32[320,640]{1,0:T(8,128)S(1)}, bf16[320,640]{1,0:T(8,128)(2,1)S(1)}) custom-call(bf16[80,640]{1,0:T(8,128)(2,1)S(1)} %collective-permute-done.2.refs_0_, bf16[80,640]{1,0:T(8,128)(2,1)S(1)} %collective-permute-done.3.refs_1_, bf16[80,640]{1,0:T(8,128)(2,1)S(1)} %collective-permute-done.4.refs_2_, ...), custom_call_target="tpu_custom_call" | custom-call | flops 2500000000 | bytes 15000000 | tf_op jit(solution)/shard_map/ffn/pallas_call | solution.py:44
  24.4 0.4 collective-permute-start.10
  24.8 1.4 %collective-permute-done.10.other_ref = bf16[320,640]{1,0:T(8,128)(2,1)S(1)} collective-permute-done((bf16[320,640]{1,0:T(8,128)(2,1)S(1)}, bf16[320,640]{1,0:T(8,128)(2,1)S(1)}, u32[]{:S(2)}, u32[]{:S(2)}) %collective-permute-start.10) | collective-permute-done | bytes 409632 | tf_op jit(solution)/shard_map/ppermute | solution.py:469
  26.2 0.1 reduce.1
  26.3 0.7 %collective-permute-start.11 = (bf16[80,640]{1,0:T(8,128)(2,1)S(1)}, bf16[80,640]{1,0:T(8,128)(2,1)S(1)}, u32[]{:S(2)}, u32[]{:S(2)}) collective-permute-start(bf16[80,640]{1,0:T(8,128)(2,1)S(1)} %get-tuple-element.30), channel_id=1, source_target_pairs={{0,0},{3,1},{2,2},{1,3},{4,4},{7,5},{6,6},{5,7},{8,8},{11,9},{10,1... | collective-permute-start | bytes 307208 | tf_op jit(solution)/shard_map/ppermute | solution.py:473
  26.9 0.5 %collective-permute-start.12 = (bf16[80,640]{1,0:T(8,128)(2,1)S(1)}, bf16[80,640]{1,0:T(8,128)(2,1)S(1)}, u32[]{:S(2)}, u32[]{:S(2)}) collective-permute-start(bf16[80,640]{1,0:T(8,128)(2,1)S(1)} %get-tuple-element.31), channel_id=1, source_target_pairs={{8,0},{11,1},{10,2},{9,3},{0,4},{3,5},{2,6},{1,7},{12,8},{15,9},{1... | collective-permute-start | bytes 307208 | tf_op jit(solution)/shard_map/ppermute | solution.py:473
  27.4 2.1 %collective-permute-start.13 = (bf16[80,640]{1,0:T(8,128)(2,1)S(1)}, bf16[80,640]{1,0:T(8,128)(2,1)S(1)}, u32[]{:S(2)}, u32[]{:S(2)}) collective-permute-start(bf16[80,640]{1,0:T(8,128)(2,1)S(1)} %get-tuple-element.32), channel_id=1, source_target_pairs={{12,0},{15,1},{14,2},{13,3},{8,4},{11,5},{10,6},{9,7},{4,8},{7,9},... | collective-permute-start | bytes 307208 | tf_op jit(solution)/shard_map/ppermute | solution.py:473
  29.5 1.9 %collective-permute-start.14 = (bf16[80,640]{1,0:T(8,128)(2,1)S(1)}, bf16[80,640]{1,0:T(8,128)(2,1)S(1)}, u32[]{:S(2)}, u32[]{:S(2)}) collective-permute-start(bf16[80,640]{1,0:T(8,128)(2,1)S(1)} %get-tuple-element.33), channel_id=1, source_target_pairs={{4,0},{7,1},{6,2},{5,3},{12,4},{15,5},{14,6},{13,7},{0,8},{3,9},{2... | collective-permute-start | bytes 307208 | tf_op jit(solution)/shard_map/ppermute | solution.py:473
  31.5 0.0 collective-permute-done.11.refs_0_
  31.5 2.9 %collective-permute-start.15 = (bf16[80,640]{1,0:T(8,128)(2,1)S(1)}, bf16[80,640]{1,0:T(8,128)(2,1)S(1)}, u32[]{:S(2)}, u32[]{:S(2)}) collective-permute-start(bf16[80,640]{1,0:T(8,128)(2,1)S(1)} %collective-permute-done.11.refs_0_), channel_id=1, source_target_pairs={{0,1},{1,0},{2,3},{3,2},{4,5},{5,4},{6,7},{7,6},{8,9},{9,8},{10,11... | collective-permute-start | bytes 307208 | tf_op jit(solution)/shard_map/ppermute | solution.py:476
  34.4 0.0 collective-permute-done.12.refs_1_
  34.4 5.6 %collective-permute-start.16 = (bf16[80,640]{1,0:T(8,128)(2,1)S(1)}, bf16[80,640]{1,0:T(8,128)(2,1)S(1)}, u32[]{:S(2)}, u32[]{:S(2)}) collective-permute-start(bf16[80,640]{1,0:T(8,128)(2,1)S(1)} %collective-permute-done.12.refs_1_), channel_id=1, source_target_pairs={{0,1},{1,0},{2,3},{3,2},{4,5},{5,4},{6,7},{7,6},{8,9},{9,8},{10,11... | collective-permute-start | bytes 307208 | tf_op jit(solution)/shard_map/ppermute | solution.py:476
  40.0 0.0 collective-permute-done.13.refs_2_
  40.0 0.0 collective-permute-start.17
  40.0 0.0 collective-permute-done.14.refs_3_
  40.0 0.5 %collective-permute-start.18 = (bf16[80,640]{1,0:T(8,128)(2,1)S(1)}, bf16[80,640]{1,0:T(8,128)(2,1)S(1)}, u32[]{:S(2)}, u32[]{:S(2)}) collective-permute-start(bf16[80,640]{1,0:T(8,128)(2,1)S(1)} %collective-permute-done.14.refs_3_), channel_id=1, source_target_pairs={{0,1},{1,0},{2,3},{3,2},{4,5},{5,4},{6,7},{7,6},{8,9},{9,8},{10,11... | collective-permute-start | bytes 307208 | tf_op jit(solution)/shard_map/ppermute | solution.py:476
  40.5 0.0 copy-done
  40.5 0.0 copy-done.1
  40.5 0.0 copy-done.2
  40.5 0.0 copy-done.3
  40.5 3.4 %attend.1 = (bf16[32,2560]{1,0:T(8,128)(2,1)}, f32[32,2560]{1,0:T(8,128)S(1)}, f32[128,128]{1,0:T(8,128)S(1)}) custom-call(s32[32]{0:T(128)} %length_ref.1, bf16[32,2560]{1,0:T(8,128)(2,1)S(1)} %copy-done.2, bf16[32,512]{1,0:T(8,128)(2,1)S(1)} %copy-done.4, bf16[32,512]{1,0:T(8,128)(2,1)S(1)} %copy-done.5, bf16[32,128,512]{2,1,0:T(8,128)(2,1)S(1)} %copy-done, ...), custom_call_target="tpu_custom_call" | custom-call | flops 2000000000 | bytes 12000000 | tf_op jit(solution)/shard_map/attend/pallas_call | solution.py:44
  44.0 0.0 collective-permute-done.15.refs_4_
  44.0 0.0 collective-permute-done.16.refs_5_
  44.0 0.0 collective-permute-done.17.refs_6_
  44.0 0.0 collective-permute-done.18.refs_7_
  44.0 0.0 copy-done.6
  44.0 1.2 %combine.1 = bf16[32,2560]{1,0:T(8,128)(2,1)} custom-call(f32[256,128]{1,0:T(8,128)S(1)} %get-tuple-element.19.pos_ref, f32[128,128]{1,0:T(8,128)S(1)} %get-tuple-element.21.weight_ref, bf16[32,2560]{1,0:T(8,128)(2,1)S(1)} %copy-done.6, f32[32,2560]{1,0:T(8,128)S(1)} %get-tuple-element.22.context_ref, bf16[80,640]{1,0:T(8,128)(2,1)S(1)} %collective-permute-done.11.refs_0_, ...), custom_call_target="tpu_custom_call" | custom-call | flops 500000000 | bytes 3000000 | tf_op jit(solution)/shard_map/combine/pallas_call | solution.py:44
  (12 shorter events, 0.0 us)
Async XLA Ops:
  0.6 2.3 %collective-permute-start.1 = (bf16[20,128]{1,0:T(8,128)(2,1)}, bf16[20,128]{1,0:T(8,128)(2,1)S(1)}, u32[]{:S(2)}, u32[]{:S(2)}) collective-permute-start(bf16[20,128]{1,0:T(8,128)(2,1)} %bitcast.7), channel_id=1, source_target_pairs={{0,1},{1,0},{2,3},{3,2},{4,5},{5,4},{6,7},{7,6},{8,9},{9,8},{10,11... | collective-permute-start | bytes 15368 | tf_op jit(solution)/shard_map/ppermute | solution.py:386
  1.2 1.8 %collective-permute-start = (bf16[32,2560]{1,0:T(8,128)(2,1)}, bf16[32,2560]{1,0:T(8,128)(2,1)S(1)}, u32[]{:S(2)}, u32[]{:S(2)}) collective-permute-start(bf16[32,2560]{1,0:T(8,128)(2,1)} %res_ref.1), channel_id=1, source_target_pairs={{0,1},{1,0},{2,3},{3,2},{4,5},{5,4},{6,7},{7,6},{8,9},{9,8},{10,11... | collective-permute-start | bytes 491528 | tf_op jit(solution)/shard_map/ppermute | solution.py:385
  1.3 18.4 %slice-start = ((s8[13107200]{0:T(1024)(128)(4,1)}), s8[4194304]{0:T(1024)(128)(4,1)S(1)}, s32[]{:S(2)}) async-start(s8[13107200]{0:T(1024)(128)(4,1)} %bitcast.2), calls=%async_computation | async-start | bytes 8388608
  1.3 18.4 %slice-start.1 = ((s8[13107200]{0:T(1024)(128)(4,1)}), s8[4194304]{0:T(1024)(128)(4,1)S(1)}, s32[]{:S(2)}) async-start(s8[13107200]{0:T(1024)(128)(4,1)} %bitcast.2), calls=%async_computation.1 | async-start | bytes 8388608
  1.3 18.4 %slice-start.4 = ((s8[13107200]{0:T(1024)(128)(4,1)}), s8[4194304]{0:T(1024)(128)(4,1)S(1)}, s32[]{:S(2)}) async-start(s8[13107200]{0:T(1024)(128)(4,1)} %bitcast.4), calls=%async_computation.4 | async-start | bytes 8388608
  1.3 18.4 %slice-start.5 = ((s8[13107200]{0:T(1024)(128)(4,1)}), s8[4194304]{0:T(1024)(128)(4,1)S(1)}, s32[]{:S(2)}) async-start(s8[13107200]{0:T(1024)(128)(4,1)} %bitcast.4), calls=%async_computation.5 | async-start | bytes 8388608
  3.0 16.7 %slice-start.2 = ((s8[13107200]{0:T(1024)(128)(4,1)}), s8[4194304]{0:T(1024)(128)(4,1)S(1)}, s32[]{:S(2)}) async-start(s8[13107200]{0:T(1024)(128)(4,1)} %bitcast.2), calls=%async_computation.2 | async-start | bytes 8388608
  3.0 16.7 %slice-start.3 = ((s8[13107200]{0:T(1024)(128)(4,1)}), s8[524288]{0:T(1024)(128)(4,1)S(1)}, s32[]{:S(2)}) async-start(s8[13107200]{0:T(1024)(128)(4,1)} %bitcast.2), calls=%async_computation.3 | async-start | bytes 1048576
  3.0 16.7 %slice-start.6 = ((s8[13107200]{0:T(1024)(128)(4,1)}), s8[4194304]{0:T(1024)(128)(4,1)S(1)}, s32[]{:S(2)}) async-start(s8[13107200]{0:T(1024)(128)(4,1)} %bitcast.4), calls=%async_computation.6 | async-start | bytes 8388608
  3.0 16.7 %slice-start.7 = ((s8[13107200]{0:T(1024)(128)(4,1)}), s8[524288]{0:T(1024)(128)(4,1)S(1)}, s32[]{:S(2)}) async-start(s8[13107200]{0:T(1024)(128)(4,1)} %bitcast.4), calls=%async_computation.7 | async-start | bytes 1048576
  3.4 8.6 %collective-permute-start.2 = (bf16[80,640]{1,0:T(8,128)(2,1)S(1)}, bf16[80,640]{1,0:T(8,128)(2,1)S(1)}, u32[]{:S(2)}, u32[]{:S(2)}) collective-permute-start(bf16[80,640]{1,0:T(8,128)(2,1)S(1)} %get-tuple-element.24), channel_id=1, source_target_pairs={{0,12},{1,15},{2,14},{3,13},{4,8},{5,11},{6,10},{7,9},{8,4},{9,7},... | collective-permute-start | bytes 307208 | tf_op jit(solution)/shard_map/ppermute | solution.py:413
  8.5 6.0 %collective-permute-start.3 = (bf16[80,640]{1,0:T(8,128)(2,1)S(1)}, bf16[80,640]{1,0:T(8,128)(2,1)S(1)}, u32[]{:S(2)}, u32[]{:S(2)}) collective-permute-start(bf16[80,640]{1,0:T(8,128)(2,1)S(1)} %get-tuple-element.25), channel_id=1, source_target_pairs={{0,8},{1,11},{2,10},{3,9},{4,0},{5,3},{6,2},{7,1},{8,12},{9,15},{1... | collective-permute-start | bytes 307208 | tf_op jit(solution)/shard_map/ppermute | solution.py:413
  8.5 9.7 %collective-permute-start.4 = (bf16[80,640]{1,0:T(8,128)(2,1)S(1)}, bf16[80,640]{1,0:T(8,128)(2,1)S(1)}, u32[]{:S(2)}, u32[]{:S(2)}) collective-permute-start(bf16[80,640]{1,0:T(8,128)(2,1)S(1)} %get-tuple-element.26), channel_id=1, source_target_pairs={{0,4},{1,7},{2,6},{3,5},{4,12},{5,15},{6,14},{7,13},{8,0},{9,3},{1... | collective-permute-start | bytes 307208 | tf_op jit(solution)/shard_map/ppermute | solution.py:413
  10.5 29.9 %copy-start = (bf16[32,128,512]{2,1,0:T(8,128)(2,1)S(1)}, bf16[32,128,512]{2,1,0:T(8,128)(2,1)}, u32[]{:S(2)}) copy-start(bf16[32,128,512]{2,1,0:T(8,128)(2,1)} %cache_key_ref.1) | copy-start | bytes 12582916
  10.5 29.9 %copy-start.1 = (bf16[32,128,512]{2,1,0:T(8,128)(2,1)S(1)}, bf16[32,128,512]{2,1,0:T(8,128)(2,1)}, u32[]{:S(2)}) copy-start(bf16[32,128,512]{2,1,0:T(8,128)(2,1)} %cache_value_ref.1) | copy-start | bytes 12582916
  10.5 29.9 %copy-start.2 = (bf16[32,2560]{1,0:T(8,128)(2,1)S(1)}, bf16[32,2560]{1,0:T(8,128)(2,1)}, u32[]{:S(2)}) copy-start(bf16[32,2560]{1,0:T(8,128)(2,1)} %query_ref.1) | copy-start | bytes 491524
  10.5 29.9 %copy-start.3 = (bf16[640,128]{1,0:T(8,128)(2,1)S(1)}, bf16[640,128]{1,0:T(8,128)(2,1)}, u32[]{:S(2)}) copy-start(bf16[640,128]{1,0:T(8,128)(2,1)} %router_ref.1) | copy-start | bytes 491524
  10.5 29.9 %copy-start.4 = (bf16[32,512]{1,0:T(8,128)(2,1)S(1)}, bf16[32,512]{1,0:T(8,128)(2,1)}, u32[]{:S(2)}) copy-start(bf16[32,512]{1,0:T(8,128)(2,1)} %key_ref.1) | copy-start | bytes 98308
  10.6 29.9 %copy-start.5 = (bf16[32,512]{1,0:T(8,128)(2,1)S(1)}, bf16[32,512]{1,0:T(8,128)(2,1)}, u32[]{:S(2)}) copy-start(bf16[32,512]{1,0:T(8,128)(2,1)} %value_ref.1) | copy-start | bytes 98308
  10.6 33.4 %copy-start.6 = (bf16[32,2560]{1,0:T(8,128)(2,1)S(1)}, bf16[32,2560]{1,0:T(8,128)(2,1)}, u32[]{:S(2)}) copy-start(bf16[32,2560]{1,0:T(8,128)(2,1)} %res_ref.1) | copy-start | bytes 491524
  10.6 7.6 %collective-permute-start.5 = (bf16[80,640]{1,0:T(8,128)(2,1)S(1)}, bf16[80,640]{1,0:T(8,128)(2,1)S(1)}, u32[]{:S(2)}, u32[]{:S(2)}) collective-permute-start(bf16[80,640]{1,0:T(8,128)(2,1)S(1)} %get-tuple-element.27), channel_id=1, source_target_pairs={{0,0},{1,3},{2,2},{3,1},{4,4},{5,7},{6,6},{7,5},{8,8},{9,11},{10,1... | collective-permute-start | bytes 307208 | tf_op jit(solution)/shard_map/ppermute | solution.py:413
  12.1 6.6 %collective-permute-start.6 = (bf16[80,640]{1,0:T(8,128)(2,1)S(1)}, bf16[80,640]{1,0:T(8,128)(2,1)S(1)}, u32[]{:S(2)}, u32[]{:S(2)}) collective-permute-start(bf16[80,640]{1,0:T(8,128)(2,1)S(1)} %collective-permute-done.2.refs_0_), channel_id=1, source_target_pairs={{0,1},{1,0},{2,3},{3,2},{4,5},{5,4},{6,7},{7,6},{8,9},{9,8},{10,11... | collective-permute-start | bytes 307208 | tf_op jit(solution)/shard_map/ppermute | solution.py:448
  14.5 4.2 %collective-permute-start.7 = (bf16[80,640]{1,0:T(8,128)(2,1)S(1)}, bf16[80,640]{1,0:T(8,128)(2,1)S(1)}, u32[]{:S(2)}, u32[]{:S(2)}) collective-permute-start(bf16[80,640]{1,0:T(8,128)(2,1)S(1)} %collective-permute-done.3.refs_1_), channel_id=1, source_target_pairs={{0,1},{1,0},{2,3},{3,2},{4,5},{5,4},{6,7},{7,6},{8,9},{9,8},{10,11... | collective-permute-start | bytes 307208 | tf_op jit(solution)/shard_map/ppermute | solution.py:448
  18.2 1.3 %collective-permute-start.8 = (bf16[80,640]{1,0:T(8,128)(2,1)S(1)}, bf16[80,640]{1,0:T(8,128)(2,1)S(1)}, u32[]{:S(2)}, u32[]{:S(2)}) collective-permute-start(bf16[80,640]{1,0:T(8,128)(2,1)S(1)} %collective-permute-done.4.refs_2_), channel_id=1, source_target_pairs={{0,1},{1,0},{2,3},{3,2},{4,5},{5,4},{6,7},{7,6},{8,9},{9,8},{10,11... | collective-permute-start | bytes 307208 | tf_op jit(solution)/shard_map/ppermute | solution.py:448
  18.2 1.5 %collective-permute-start.9 = (bf16[80,640]{1,0:T(8,128)(2,1)S(1)}, bf16[80,640]{1,0:T(8,128)(2,1)S(1)}, u32[]{:S(2)}, u32[]{:S(2)}) collective-permute-start(bf16[80,640]{1,0:T(8,128)(2,1)S(1)} %collective-permute-done.5.refs_3_), channel_id=1, source_target_pairs={{0,1},{1,0},{2,3},{3,2},{4,5},{5,4},{6,7},{7,6},{8,9},{9,8},{10,11... | collective-permute-start | bytes 307208 | tf_op jit(solution)/shard_map/ppermute | solution.py:448
  24.4 1.8 %collective-permute-start.10 = (bf16[320,640]{1,0:T(8,128)(2,1)S(1)}, bf16[320,640]{1,0:T(8,128)(2,1)S(1)}, u32[]{:S(2)}, u32[]{:S(2)}) collective-permute-start(bf16[320,640]{1,0:T(8,128)(2,1)S(1)} %get-tuple-element.29), channel_id=1, source_target_pairs={{0,1},{1,0},{2,3},{3,2},{4,5},{5,4},{6,7},{7,6},{8,9},{9,8},{10,11... | collective-permute-start | bytes 1228808 | tf_op jit(solution)/shard_map/ppermute | solution.py:469
  26.3 5.2 %collective-permute-start.11 = (bf16[80,640]{1,0:T(8,128)(2,1)S(1)}, bf16[80,640]{1,0:T(8,128)(2,1)S(1)}, u32[]{:S(2)}, u32[]{:S(2)}) collective-permute-start(bf16[80,640]{1,0:T(8,128)(2,1)S(1)} %get-tuple-element.30), channel_id=1, source_target_pairs={{0,0},{3,1},{2,2},{1,3},{4,4},{7,5},{6,6},{5,7},{8,8},{11,9},{10,1... | collective-permute-start | bytes 307208 | tf_op jit(solution)/shard_map/ppermute | solution.py:473
  26.9 7.4 %collective-permute-start.12 = (bf16[80,640]{1,0:T(8,128)(2,1)S(1)}, bf16[80,640]{1,0:T(8,128)(2,1)S(1)}, u32[]{:S(2)}, u32[]{:S(2)}) collective-permute-start(bf16[80,640]{1,0:T(8,128)(2,1)S(1)} %get-tuple-element.31), channel_id=1, source_target_pairs={{8,0},{11,1},{10,2},{9,3},{0,4},{3,5},{2,6},{1,7},{12,8},{15,9},{1... | collective-permute-start | bytes 307208 | tf_op jit(solution)/shard_map/ppermute | solution.py:473
  27.4 12.5 %collective-permute-start.13 = (bf16[80,640]{1,0:T(8,128)(2,1)S(1)}, bf16[80,640]{1,0:T(8,128)(2,1)S(1)}, u32[]{:S(2)}, u32[]{:S(2)}) collective-permute-start(bf16[80,640]{1,0:T(8,128)(2,1)S(1)} %get-tuple-element.32), channel_id=1, source_target_pairs={{12,0},{15,1},{14,2},{13,3},{8,4},{11,5},{10,6},{9,7},{4,8},{7,9},... | collective-permute-start | bytes 307208 | tf_op jit(solution)/shard_map/ppermute | solution.py:473
  29.5 10.4 %collective-permute-start.14 = (bf16[80,640]{1,0:T(8,128)(2,1)S(1)}, bf16[80,640]{1,0:T(8,128)(2,1)S(1)}, u32[]{:S(2)}, u32[]{:S(2)}) collective-permute-start(bf16[80,640]{1,0:T(8,128)(2,1)S(1)} %get-tuple-element.33), channel_id=1, source_target_pairs={{4,0},{7,1},{6,2},{5,3},{12,4},{15,5},{14,6},{13,7},{0,8},{3,9},{2... | collective-permute-start | bytes 307208 | tf_op jit(solution)/shard_map/ppermute | solution.py:473
  31.5 12.5 %collective-permute-start.15 = (bf16[80,640]{1,0:T(8,128)(2,1)S(1)}, bf16[80,640]{1,0:T(8,128)(2,1)S(1)}, u32[]{:S(2)}, u32[]{:S(2)}) collective-permute-start(bf16[80,640]{1,0:T(8,128)(2,1)S(1)} %collective-permute-done.11.refs_0_), channel_id=1, source_target_pairs={{0,1},{1,0},{2,3},{3,2},{4,5},{5,4},{6,7},{7,6},{8,9},{9,8},{10,11... | collective-permute-start | bytes 307208 | tf_op jit(solution)/shard_map/ppermute | solution.py:476
  34.4 9.6 %collective-permute-start.16 = (bf16[80,640]{1,0:T(8,128)(2,1)S(1)}, bf16[80,640]{1,0:T(8,128)(2,1)S(1)}, u32[]{:S(2)}, u32[]{:S(2)}) collective-permute-start(bf16[80,640]{1,0:T(8,128)(2,1)S(1)} %collective-permute-done.12.refs_1_), channel_id=1, source_target_pairs={{0,1},{1,0},{2,3},{3,2},{4,5},{5,4},{6,7},{7,6},{8,9},{9,8},{10,11... | collective-permute-start | bytes 307208 | tf_op jit(solution)/shard_map/ppermute | solution.py:476
  40.0 4.0 %collective-permute-start.17 = (bf16[80,640]{1,0:T(8,128)(2,1)S(1)}, bf16[80,640]{1,0:T(8,128)(2,1)S(1)}, u32[]{:S(2)}, u32[]{:S(2)}) collective-permute-start(bf16[80,640]{1,0:T(8,128)(2,1)S(1)} %collective-permute-done.13.refs_2_), channel_id=1, source_target_pairs={{0,1},{1,0},{2,3},{3,2},{4,5},{5,4},{6,7},{7,6},{8,9},{9,8},{10,11... | collective-permute-start | bytes 307208 | tf_op jit(solution)/shard_map/ppermute | solution.py:476
  40.0 4.0 %collective-permute-start.18 = (bf16[80,640]{1,0:T(8,128)(2,1)S(1)}, bf16[80,640]{1,0:T(8,128)(2,1)S(1)}, u32[]{:S(2)}, u32[]{:S(2)}) collective-permute-start(bf16[80,640]{1,0:T(8,128)(2,1)S(1)} %collective-permute-done.14.refs_3_), channel_id=1, source_target_pairs={{0,1},{1,0},{2,3},{3,2},{4,5},{5,4},{6,7},{7,6},{8,9},{9,8},{10,11... | collective-permute-start | bytes 307208 | tf_op jit(solution)/shard_map/ppermute | solution.py:476
